TPU v7x, 128 devices: a whole 4x4x4 slice. The times are simulated.
128 devices in a mesh: dp: 1, ep: 128 (over z, y, x, core).
Axes of the slice: x: 4, y: 4, z: 4, core: 2. Of those that a mesh axis runs over, the one named last changes fastest.
Arguments:
- x_a: bfloat16 [4096, 2048], P(('dp', 'ep'))
- route_a: int32 [4096, 8], P(('dp', 'ep'))
- gate_a: float32 [4096, 8], P(('dp', 'ep'))
- h_b: bfloat16 [4096, 2048], P(('dp', 'ep'))
- attn_b: bfloat16 [4096, 4096], P(('dp', 'ep'))
- route_b: int32 [4096, 8], P(('dp', 'ep'))
- gate_b: float32 [4096, 8], P(('dp', 'ep'))
- w_qkv: bfloat16 [2048, 5120], replicated
- w_o: bfloat16 [4096, 2048], replicated
- w_gate: bfloat16 [128, 2048, 768], P('ep')
- w_up: bfloat16 [128, 2048, 768], P('ep')
- w_down: bfloat16 [128, 768, 2048], P('ep')
Outputs:
- output 1: bfloat16 [4096, 2048], P(('dp', 'ep'))
- output 2: bfloat16 [4096, 2048], P(('dp', 'ep'))
- output 3: bfloat16 [4096, 5120], P(('dp', 'ep'))
All inputs are finite; a program needn't handle non-finite values.
Results may differ from a plain program's by a relative error of at most 0.0107943.
Values are sent between devices in bfloat16 or wider.
A program may use at most 1 GiB of HBM per device.

v0:
```python
import jax
import jax.numpy as jnp
from jax import lax
from jax.sharding import PartitionSpec as P


def route_slots(route_ids, n_experts, n_devs, capacity):
    tok_n, top_k = route_ids.shape
    local_n = n_experts // n_devs
    flat_route = route_ids.reshape(tok_n * top_k)
    one_hot = (flat_route[:, None] == jnp.arange(n_experts)[None, :]).astype(jnp.int32)
    slot_rank = jnp.sum((jnp.cumsum(one_hot, axis=0) - 1) * one_hot, axis=1)
    owner = flat_route // local_n
    local_id = flat_route % local_n
    slot_ids = local_id * (n_devs * capacity) + owner * capacity + slot_rank
    return slot_ids.reshape(tok_n, top_k)


def expert_ffn(rows_in, w_gate, w_up, w_down):
    gate_act = jnp.einsum('erd,edf->erf', rows_in, w_gate, preferred_element_type=jnp.float32)
    up_act = jnp.einsum('erd,edf->erf', rows_in, w_up, preferred_element_type=jnp.float32)
    hidden = (jax.nn.silu(gate_act) * up_act).astype(jnp.bfloat16)
    return jnp.einsum('erf,efd->erd', hidden, w_down, preferred_element_type=jnp.float32).astype(jnp.bfloat16)


def moe_local(tokens, route_ids, gate_vals, w_gate, w_up, w_down, n_devs):
    tok_n, model_dim = tokens.shape
    top_k = route_ids.shape[1]
    local_n = w_gate.shape[0]
    n_experts = local_n * n_devs
    capacity = min(tok_n, 2 * ((tok_n * top_k + n_experts - 1) // n_experts))
    n_slots = n_experts * capacity
    slot_ids = route_slots(route_ids, n_experts, n_devs, capacity)
    picker = (slot_ids[:, :, None] == jnp.arange(n_slots)[None, None, :]).astype(jnp.bfloat16)
    placer = jnp.sum(picker, axis=1)
    send_buf = jnp.einsum('ts,td->sd', placer, tokens, preferred_element_type=jnp.float32).astype(jnp.bfloat16)
    send_buf = send_buf.reshape(local_n, n_devs, capacity, model_dim)
    recv_buf = lax.all_to_all(send_buf, 'ep', 1, 1, tiled=True)
    expert_out = expert_ffn(recv_buf.reshape(local_n, n_devs * capacity, model_dim), w_gate, w_up, w_down)
    back_buf = lax.all_to_all(expert_out.reshape(local_n, n_devs, capacity, model_dim), 'ep', 1, 1, tiled=True)
    picked = jnp.einsum('tjs,sd->tjd', picker, back_buf.reshape(n_slots, model_dim), preferred_element_type=jnp.float32)
    mixture = jnp.zeros((tok_n, model_dim), jnp.float32)
    for choice in range(top_k):
        mixture = mixture + gate_vals[:, choice:choice + 1] * picked[:, choice]
    return (tokens.astype(jnp.float32) + mixture).astype(jnp.bfloat16)


def solution(mesh):
    n_devs = mesh.shape['ep']

    def local_step(x_a, route_a, gate_a, h_b, attn_b, route_b, gate_b, w_qkv, w_o, w_gate, w_up, w_down):
        out_a = moe_local(x_a, route_a, gate_a, w_gate, w_up, w_down, n_devs)
        qkv_b = jnp.dot(h_b, w_qkv, preferred_element_type=jnp.float32).astype(jnp.bfloat16)
        proj_b = jnp.dot(attn_b, w_o, preferred_element_type=jnp.float32).astype(jnp.bfloat16)
        mid_b = (h_b.astype(jnp.float32) + proj_b.astype(jnp.float32)).astype(jnp.bfloat16)
        out_b = moe_local(mid_b, route_b, gate_b, w_gate, w_up, w_down, n_devs)
        return out_a, out_b, qkv_b

    row_spec = P(('dp', 'ep'), None)
    full_spec = P(None, None)
    expert_spec = P('ep', None, None)
    return jax.shard_map(
        local_step,
        mesh=mesh,
        in_specs=(row_spec, row_spec, row_spec, row_spec, row_spec, row_spec, row_spec, full_spec, full_spec, expert_spec, expert_spec, expert_spec),
        out_specs=(row_spec, row_spec, row_spec),
        check_vma=False,
    )
```

profile of v0, /device:TPU:0, one launch (start us, length us, event | category | flops | bytes accessed | tf_op | source)
XLA Modules:
  0.0 171.7 jit_solution(14455964276540885869)
XLA Ops:
  2.7 3.0 %convolution_convert_fusion.2 = bf16[512,2048]{1,0:T(8,128)(2,1)} fusion(bf16[32,512]{1,0:T(8,128)(2,1)S(1)} %fusion.33, bf16[32,2048]{1,0:T(8,128)(2,1)} %param.12), kind=kOutput, calls=%fused_computation.16 | convolution fusion | flops 68157440 | bytes 2260992 | tf_op jit(solution)/shard_map/ts,td->sd/dot_general | solution.py:36
  5.7 4.1 %reshape.132 = bf16[1,128,4,2048]{3,2,1,0:T(4,128)(2,1)} reshape(bf16[512,2048]{1,0:T(8,128)(2,1)} %convolution_convert_fusion.2) | data formatting | bytes 4194304 | tf_op jit(solution)/shard_map/reshape | solution.py:37
  9.8 11.7 %all-to-all-start = ((bf16[1,128,4,2048]{3,2,0,1:T(4,128)(2,1)}), bf16[1,128,4,2048]{3,2,0,1:T(4,128)(2,1)}, u32[]{:S(2)}, u32[]{:S(2)}) async-start(bf16[1,128,4,2048]{3,2,0,1:T(4,128)(2,1)} %bitcast.228), calls=%async_computation | async-start | bytes 4194304 | tf_op jit(solution)/shard_map/all_to_all | solution.py:38
  22.8 8.9 %fusion.20 = bf16[32,2048]{1,0:T(8,128)(2,1)S(1)} fusion(bf16[32,4096]{1,0:T(8,128)(2,1)} %param.16, bf16[4096,2048]{1,0:T(8,128)(2,1)} %param.20, bf16[32,2048]{1,0:T(8,128)(2,1)S(1)} %copy-done.9), kind=kOutput, calls=%fused_computation.20 | convolution fusion | flops 537198592 | bytes 17301504 | tf_op jit(solution)/shard_map/dot_general | solution.py:54
  33.7 4.1 %reshape.140 = bf16[1,128,4,2048]{3,2,1,0:T(4,128)(2,1)} reshape(bf16[512,2048]{1,0:T(8,128)(2,1)} %convolution_convert_fusion.1) | data formatting | bytes 4194304 | tf_op jit(solution)/shard_map/reshape | solution.py:37
  37.8 15.1 %all-to-all-done = bf16[1,128,4,2048]{3,2,0,1:T(4,128)(2,1)} async-done(((bf16[1,128,4,2048]{3,2,0,1:T(4,128)(2,1)}), bf16[1,128,4,2048]{3,2,0,1:T(4,128)(2,1)}, u32[]{:S(2)}, u32[]{:S(2)}) %all-to-all-start) | async-done | bytes 2097184 | tf_op jit(solution)/shard_map/all_to_all | solution.py:38
  53.0 5.8 %all-to-all-start.2 = ((bf16[1,128,4,2048]{3,2,0,1:T(4,128)(2,1)}), bf16[1,128,4,2048]{3,2,0,1:T(4,128)(2,1)}, u32[]{:S(2)}, u32[]{:S(2)}) async-start(bf16[1,128,4,2048]{3,2,0,1:T(4,128)(2,1)} %bitcast.229), calls=%async_computation.2 | async-start | bytes 4194304 | tf_op jit(solution)/shard_map/all_to_all | solution.py:38
  58.8 4.0 %reshape.133 = bf16[512,2048]{1,0:T(8,128)(2,1)} reshape(bf16[1,128,4,2048]{3,2,0,1:T(4,128)(2,1)} %all-to-all-done) | data formatting | bytes 4194304 | tf_op jit(solution)/shard_map/reshape.6
  62.7 5.5 %fusion.10 = f32[512,768]{1,0:T(8,128)} fusion(bf16[512,2048]{1,0:T(8,128)(2,1)} %reshape.133, bf16[1,2048,768]{2,1,0:T(8,128)(2,1)} %param.21), kind=kOutput, calls=%fused_computation.11 | convolution fusion | flops 1610612736 | bytes 6815744 | tf_op jit(solution)/shard_map/erd,edf->erf/dot_general | solution.py:20
  68.2 8.3 %fusion.12 = bf16[512,2048]{1,0:T(8,128)(2,1)} fusion(bf16[1,768,2048]{2,1,0:T(8,128)(2,1)S(1)} %copy-done, f32[512,768]{1,0:T(8,128)} %fusion.10, bf16[512,2048]{1,0:T(8,128)(2,1)} %reshape.133, bf16[1,2048,768]{2,1,0:T(8,128)(2,1)} %param.22), kind=kOutput, calls=%fused_computation.13 | convolution fusion | flops 3224633344 | bytes 12058624 | tf_op jit(solution)/shard_map/erf,efd->erd/dot_general | solution.py:23
  76.5 4.1 %reshape.137 = bf16[1,128,4,2048]{3,2,1,0:T(4,128)(2,1)} reshape(bf16[512,2048]{1,0:T(8,128)(2,1)} %fusion.12) | data formatting | bytes 4194304 | tf_op jit(solution)/shard_map/reshape | solution.py:40
  80.6 9.6 %all-to-all-done.2 = bf16[1,128,4,2048]{3,2,0,1:T(4,128)(2,1)} async-done(((bf16[1,128,4,2048]{3,2,0,1:T(4,128)(2,1)}), bf16[1,128,4,2048]{3,2,0,1:T(4,128)(2,1)}, u32[]{:S(2)}, u32[]{:S(2)}) %all-to-all-start.2) | async-done | bytes 2097184 | tf_op jit(solution)/shard_map/all_to_all | solution.py:38
  90.2 6.1 %all-to-all-start.1 = ((bf16[1,128,4,2048]{3,2,0,1:T(4,128)(2,1)}), bf16[1,128,4,2048]{3,2,0,1:T(4,128)(2,1)}, u32[]{:S(2)}, u32[]{:S(2)}) async-start(bf16[1,128,4,2048]{3,2,0,1:T(4,128)(2,1)} %bitcast.227), calls=%async_computation.1 | async-start | bytes 4194304 | tf_op jit(solution)/shard_map/all_to_all | solution.py:40
  98.3 4.0 %reshape.141 = bf16[512,2048]{1,0:T(8,128)(2,1)} reshape(bf16[1,128,4,2048]{3,2,0,1:T(4,128)(2,1)} %all-to-all-done.2) | data formatting | bytes 4194304 | tf_op jit(solution)/shard_map/reshape.29
  102.3 5.5 %fusion.8 = f32[512,768]{1,0:T(8,128)} fusion(bf16[512,2048]{1,0:T(8,128)(2,1)} %reshape.141, bf16[1,2048,768]{2,1,0:T(8,128)(2,1)} %param.21), kind=kOutput, calls=%fused_computation.9 | convolution fusion | flops 1610612736 | bytes 6815744 | tf_op jit(solution)/shard_map/erd,edf->erf/dot_general | solution.py:20
  107.8 8.3 %fusion.15 = bf16[512,2048]{1,0:T(8,128)(2,1)} fusion(bf16[1,768,2048]{2,1,0:T(8,128)(2,1)S(1)} %copy-done, f32[512,768]{1,0:T(8,128)} %fusion.8, bf16[512,2048]{1,0:T(8,128)(2,1)} %reshape.141, bf16[1,2048,768]{2,1,0:T(8,128)(2,1)} %param.22), kind=kOutput, calls=%fused_computation.14 | convolution fusion | flops 3224633344 | bytes 12058624 | tf_op jit(solution)/shard_map/erf,efd->erd/dot_general | solution.py:23
  116.1 4.1 %reshape.142 = bf16[1,128,4,2048]{3,2,1,0:T(4,128)(2,1)} reshape(bf16[512,2048]{1,0:T(8,128)(2,1)} %fusion.15) | data formatting | bytes 4194304 | tf_op jit(solution)/shard_map/reshape | solution.py:40
  120.2 7.5 %all-to-all-done.1 = bf16[1,128,4,2048]{3,2,0,1:T(4,128)(2,1)} async-done(((bf16[1,128,4,2048]{3,2,0,1:T(4,128)(2,1)}), bf16[1,128,4,2048]{3,2,0,1:T(4,128)(2,1)}, u32[]{:S(2)}, u32[]{:S(2)}) %all-to-all-start.1) | async-done | bytes 2097184 | tf_op jit(solution)/shard_map/all_to_all | solution.py:40
  127.7 4.9 %all-to-all-start.3 = ((bf16[1,128,4,2048]{3,2,0,1:T(4,128)(2,1)}), bf16[1,128,4,2048]{3,2,0,1:T(4,128)(2,1)S(1)}, u32[]{:S(2)}, u32[]{:S(2)}) async-start(bf16[1,128,4,2048]{3,2,0,1:T(4,128)(2,1)} %bitcast.28), calls=%async_computation.3 | async-start | bytes 4194304 | tf_op jit(solution)/shard_map/all_to_all | solution.py:40
  132.6 9.6 %convolution_convert_fusion = bf16[32,5120]{1,0:T(8,128)(2,1)} fusion(bf16[32,2048]{1,0:T(8,128)(2,1)S(1)} %copy-done.9, bf16[2048,5120]{1,0:T(8,128)(2,1)} %param.19), kind=kOutput, calls=%fused_computation | convolution fusion | flops 671252480 | bytes 21430272 | tf_op jit(solution)/shard_map/dot_general | solution.py:53
  142.2 3.9 %reshape.144 = bf16[512,2048,1]{1,0,2:T(8,128)(2,1)} reshape(bf16[1,128,4,2048]{3,2,0,1:T(4,128)(2,1)} %all-to-all-done.1) | data formatting | bytes 4194304 | tf_op jit(solution)/shard_map/reshape | solution.py:41
  146.2 2.3 %fusion.29 = f32[32,8,2048]{2,1,0:T(8,128)S(1)} fusion(bf16[512,2048,1]{1,0,2:T(8,128)(2,1)} %reshape.144, s32[32,8]{1,0:T(8,128)S(1)} %multiply_add_fusion.1), kind=kOutput, calls=%fused_computation.25 | convolution fusion | flops 537001984 | bytes 4195328 | tf_op jit(solution)/shard_map/tjs,sd->tjd/dot_general | solution.py:41
  148.5 2.6 %fusion.78 = (f32[32,1,2048]{2,1,0:T(1,128)S(1)}, f32[32,1,2048]{2,1,0:T(1,128)}, f32[32,1,2048]{2,1,0:T(1,128)}, f32[32,1,2048]{2,1,0:T(1,128)}, f32[32,1,2048]...) fusion(f32[32,8,2048]{2,1,0:T(8,128)S(1)} %fusion.29), kind=kLoop, calls=%fused_computation.119 | loop fusion | bytes 4194304 | tf_op jit(solution)/shard_map/slice | solution.py:44
  151.1 12.9 %all-to-all-done.3 = bf16[1,128,4,2048]{3,2,0,1:T(4,128)(2,1)S(1)} async-done(((bf16[1,128,4,2048]{3,2,0,1:T(4,128)(2,1)}), bf16[1,128,4,2048]{3,2,0,1:T(4,128)(2,1)S(1)}, u32[]{:S(2)}, u32[]{:S(2)}) %all-to-all-start.3) | async-done | bytes 2097184 | tf_op jit(solution)/shard_map/all_to_all | solution.py:40
  (90 shorter events, 14.7 us)
Async XLA Ops:
  0.6 67.6 %copy-start = (bf16[1,768,2048]{2,1,0:T(8,128)(2,1)S(1)}, bf16[1,768,2048]{2,1,0:T(8,128)(2,1)}, u32[]{:S(2)}) copy-start(bf16[1,768,2048]{2,1,0:T(8,128)(2,1)} %param.23) | copy-start | bytes 9437188
  9.8 11.8 %copy-start.12 = (s32[32,8]{0,1:T(8,128)S(1)}, s32[32,8]{0,1:T(8,128)}, u32[]{:S(2)}) copy-start(s32[32,8]{0,1:T(8,128)} %param.17) | copy-start | bytes 3076
  9.8 13.0 %copy-start.9 = (bf16[32,2048]{1,0:T(8,128)(2,1)S(1)}, bf16[32,2048]{1,0:T(8,128)(2,1)}, u32[]{:S(2)}) copy-start(bf16[32,2048]{1,0:T(8,128)(2,1)} %param.15) | copy-start | bytes 393220
  9.8 43.2 %all-to-all-start = ((bf16[1,128,4,2048]{3,2,0,1:T(4,128)(2,1)}), bf16[1,128,4,2048]{3,2,0,1:T(4,128)(2,1)}, u32[]{:S(2)}, u32[]{:S(2)}) async-start(bf16[1,128,4,2048]{3,2,0,1:T(4,128)(2,1)} %bitcast.228), calls=%async_computation | async-start | bytes 4194304 | tf_op jit(solution)/shard_map/all_to_all | solution.py:38
  53.0 37.2 %all-to-all-start.2 = ((bf16[1,128,4,2048]{3,2,0,1:T(4,128)(2,1)}), bf16[1,128,4,2048]{3,2,0,1:T(4,128)(2,1)}, u32[]{:S(2)}, u32[]{:S(2)}) async-start(bf16[1,128,4,2048]{3,2,0,1:T(4,128)(2,1)} %bitcast.229), calls=%async_computation.2 | async-start | bytes 4194304 | tf_op jit(solution)/shard_map/all_to_all | solution.py:38
  90.2 6.1 %copy-start.13 = (f32[32,8]{0,1:T(8,128)S(1)}, f32[32,8]{0,1:T(8,128)}, u32[]{:S(2)}) copy-start(f32[32,8]{0,1:T(8,128)} %param.14) | copy-start | bytes 3076
  90.2 6.7 %copy-start.14 = (f32[32,8]{0,1:T(8,128)S(1)}, f32[32,8]{0,1:T(8,128)}, u32[]{:S(2)}) copy-start(f32[32,8]{0,1:T(8,128)} %param.18) | copy-start | bytes 3076
  90.2 37.5 %all-to-all-start.1 = ((bf16[1,128,4,2048]{3,2,0,1:T(4,128)(2,1)}), bf16[1,128,4,2048]{3,2,0,1:T(4,128)(2,1)}, u32[]{:S(2)}, u32[]{:S(2)}) async-start(bf16[1,128,4,2048]{3,2,0,1:T(4,128)(2,1)} %bitcast.227), calls=%async_computation.1 | async-start | bytes 4194304 | tf_op jit(solution)/shard_map/all_to_all | solution.py:40
  127.7 36.3 %all-to-all-start.3 = ((bf16[1,128,4,2048]{3,2,0,1:T(4,128)(2,1)}), bf16[1,128,4,2048]{3,2,0,1:T(4,128)(2,1)S(1)}, u32[]{:S(2)}, u32[]{:S(2)}) async-start(bf16[1,128,4,2048]{3,2,0,1:T(4,128)(2,1)} %bitcast.28), calls=%async_computation.3 | async-start | bytes 4194304 | tf_op jit(solution)/shard_map/all_to_all | solution.py:40
  151.1 15.0 %copy-start.11 = (pred[32,8,512]{2,1,0:T(8,128)(4,1)S(1)}, pred[32,8,512]{2,1,0:T(8,128)(4,1)}, u32[]{:S(2)}) copy-start(pred[32,8,512]{2,1,0:T(8,128)(4,1)} %iota_compare_fusion) | copy-start | bytes 393220
  166.1 2.5 %copy-start.19 = (f32[32]{0:T(128)S(1)}, f32[32]{0:T(128)}, u32[]{:S(2)}) copy-start(f32[32]{0:T(128)} %get-tuple-element.11) | copy-start | bytes 388
  166.1 2.5 %copy-start.20 = (f32[32]{0:T(128)S(1)}, f32[32]{0:T(128)}, u32[]{:S(2)}) copy-start(f32[32]{0:T(128)} %get-tuple-element.12) | copy-start | bytes 388
  166.1 2.5 %copy-start.21 = (f32[32]{0:T(128)S(1)}, f32[32]{0:T(128)}, u32[]{:S(2)}) copy-start(f32[32]{0:T(128)} %get-tuple-element.13) | copy-start | bytes 388
  166.1 2.5 %copy-start.22 = (f32[32]{0:T(128)S(1)}, f32[32]{0:T(128)}, u32[]{:S(2)}) copy-start(f32[32]{0:T(128)} %get-tuple-element.14) | copy-start | bytes 388
  166.1 2.5 %copy-start.23 = (f32[32]{0:T(128)S(1)}, f32[32]{0:T(128)}, u32[]{:S(2)}) copy-start(f32[32]{0:T(128)} %get-tuple-element.15) | copy-start | bytes 388
  166.1 2.5 %copy-start.24 = (f32[32]{0:T(128)S(1)}, f32[32]{0:T(128)}, u32[]{:S(2)}) copy-start(f32[32]{0:T(128)} %get-tuple-element.16) | copy-start | bytes 388
  166.1 2.5 %copy-start.25 = (f32[32]{0:T(128)S(1)}, f32[32]{0:T(128)}, u32[]{:S(2)}) copy-start(f32[32]{0:T(128)} %get-tuple-element.17) | copy-start | bytes 388
  166.1 2.5 %copy-start.26 = (f32[32]{0:T(128)S(1)}, f32[32]{0:T(128)}, u32[]{:S(2)}) copy-start(f32[32]{0:T(128)} %get-tuple-element.18) | copy-start | bytes 388
  168.5 1.4 copy-start.8
  168.5 1.4 copy-start.10
  168.5 1.4 copy-start.15
  168.6 1.4 copy-start.16
  168.6 1.4 copy-start.17
  168.6 3.1 %copy-start.1 = (bf16[1,768,2048]{2,1,0:T(8,128)(2,1)S(1)}, bf16[1,768,2048]{2,1,0:T(8,128)(2,1)}, u32[]{:S(2)}) copy-start(bf16[1,768,2048]{2,1,0:T(8,128)(2,1)} %param.23) | copy-start | bytes 9437188
  (7 other events, 8.4 us)
where the time goes:
time: 173 us; the launch traced here: 172 us
  matrix products  55.7 us (32%)
  waiting for transfers between devices  45.1 us (26%)
  local copies, waits for them, and re-layouts  36.5 us (21%)
  starting transfers between devices  28.5 us (16%)
  other arithmetic  4.83 us (3%)
    all_to_all x2, waiting for transfers between devices, moe_local(): recv_buf = lax.all_to_all(send_buf, 'ep', 1, 1, tiled=True)  24.7 us
    all_to_all x2, waiting for transfers between devices, moe_local(): lax.all_to_all(expert_out.reshape(local_n, n_devs, capacity, model_dim),...  20.5 us
    all_to_all x2, starting transfers between devices, moe_local(): recv_buf = lax.all_to_all(send_buf, 'ep', 1, 1, tiled=True)  17.5 us
    dot_general x2, matrix products, expert_ffn(): jnp.einsum('erf,efd->erd', hidden, w_down, preferred_element_type=jnp.flo...  16.6 us
    all_to_all x2, starting transfers between devices, moe_local(): lax.all_to_all(expert_out.reshape(local_n, n_devs, capacity, model_dim),...  11 us
    dot_general x2, matrix products, expert_ffn(): jnp.einsum('erd,edf->erf', rows_in, w_gate, preferred_element_type=jnp.fl...  11 us
    dot_general x1, matrix products, local_step(): jnp.dot(h_b, w_qkv, preferred_element_type=jnp.float32).astype(jnp.bfloat16)  9.63 us
    dot_general x1, matrix products, local_step(): jnp.dot(attn_b, w_o, preferred_element_type=jnp.float32)  8.85 us
  transfers between devices with their start and end apart: 4, of which 4 were waited for; matrix products, arithmetic and copies ran while one was open for 47% of the time, Pallas kernels for 0%

commit v1 on v0

v1 whole, which is shorter than its diff:
```python
import functools

import jax
import jax.numpy as jnp
from jax import lax
from jax.experimental import pallas as pl
from jax.experimental.pallas import tpu as pltpu
from jax.sharding import PartitionSpec as P

MESH = pl.DeviceIdType.MESH
BF16 = jnp.bfloat16
F32 = jnp.float32

SIDE = 4
CORES = 2
TOK = 32
CAP = 4
TOP_K = 8
D = 2048
N_EXP = 128
FF = 768
ATT = 4096
QKV = 5120
SLOTS = N_EXP * CAP
CLASSES = ((0, 1, 2), (1, 2, 0), (2, 0, 1))
WIDTHS = (768, 640, 640)
STARTS = (0, 768, 1408)
STRIDE = (32, 8, 2)
UNUSED = 8.0
WO_CHUNK = 512
WQ_CHUNK = 256


def iota(shape, dim):
    return lax.broadcasted_iota(jnp.int32, shape, dim)


def dot(a, b):
    return jnp.dot(a, b, preferred_element_type=F32)


def dot_nt(a, b):
    return lax.dot_general(a, b, (((1,), (1,)), ((), ())), preferred_element_type=F32)


def slot_fields(cls, idx):
    d1, d2, d3 = CLASSES[cls]
    out = {d3: idx >> 7, d2: (idx >> 4) & 3, d1: (idx >> 2) & 3}
    return out, (idx >> 6) & 1, idx & 3


def slot_index(cls, coords, core, rank):
    d1, d2, d3 = CLASSES[cls]
    return (coords[d3] << 7) | (core << 6) | (coords[d2] << 4) | (coords[d1] << 2) | rank


def reorder(to_cls, from_cls):
    row = iota((SLOTS, 1), 0)
    coords, core, rank = slot_fields(to_cls, row)
    want = slot_index(from_cls, coords, core, rank)
    return (iota((SLOTS, SLOTS), 1) == want).astype(F32).astype(BF16)


class Links:
    def __init__(self, send, recv):
        self.send, self.recv, self.used, self.open = send, recv, 0, []

    def copy(self, src, dst, device):
        i = self.used
        self.used += 1
        op = pltpu.make_async_remote_copy(
            src_ref=src, dst_ref=dst, send_sem=self.send.at[i], recv_sem=self.recv.at[i],
            device_id={"ep": device}, device_id_type=MESH)
        op.start()
        self.open.append(op)
        return op

    def drain(self):
        for op in self.open:
            op.wait_send()


def n_copies():
    return 2 * (9 + 9 + 9 + 21 + 21 + 9 + 9)


def kernel(*refs):
    it = iter(refs)
    take = lambda n: [next(it) for _ in range(n)]
    x_a, h_b, attn, route_a, route_b, gate_a, gate_b = take(7)
    w_qkv, w_o, w_gate, w_up, w_down = take(5)
    out_a, out_b, qkv_out = take(3)
    bufs = []
    for _ in range(2):
        b = {}
        for name in ("ag", "ps", "pr", "r1", "r2", "sm", "r3", "gg"):
            b[name] = take(3)
        bufs.append(b)
    xbuf, hbuf, perms, proj_acc, qkv_acc, u_b = take(6)
    vg, vu, vd, wo_buf, wq_buf = take(5)
    send_sem, recv_sem, w_sem, wo_sem, wq_sem = take(5)

    me = lax.axis_index("ep")
    core = lax.rem(me, 2)
    pos = [lax.rem(me // 32, 4), lax.rem(me // 8, 4), lax.rem(me // 2, 4)]
    links = Links(send_sem, recv_sem)

    def along(dim, off):
        there = lax.rem(pos[dim] + off, 4)
        return there, me + (there - pos[dim]) * STRIDE[dim]

    peers = []
    for dim in range(3):
        for off in (1, 2, 3):
            _, dev = along(dim, off)
            peers += [dev, dev + 1 - 2 * core]
    peers.append(me + 1 - 2 * core)
    barrier = pltpu.get_barrier_semaphore()
    for dev in peers:
        pl.semaphore_signal(barrier, inc=1, device_id={"ep": dev}, device_id_type=MESH)

    w_copies = [pltpu.make_async_copy(src.at[0], dst, w_sem.at[i])
                for i, (src, dst) in enumerate(((w_gate, vg), (w_up, vu), (w_down, vd)))]
    n_wo, n_wq = ATT // WO_CHUNK, D // WQ_CHUNK

    def wo_copy(i):
        return pltpu.make_async_copy(w_o.at[pl.ds(i * WO_CHUNK, WO_CHUNK)], wo_buf.at[i % 2], wo_sem.at[i % 2])

    def wq_copy(i):
        return pltpu.make_async_copy(w_qkv.at[pl.ds(i * WQ_CHUNK, WQ_CHUNK)], wq_buf.at[i % 2], wq_sem.at[i % 2])

    wo_copy(0).start()
    wo_copy(1).start()
    for c in w_copies:
        c.start()
    wq_copy(0).start()
    wq_copy(1).start()

    def proj_step(i):
        wo_copy(i).wait()
        part = dot(attn[:, i * WO_CHUNK:(i + 1) * WO_CHUNK], wo_buf[i % 2])
        proj_acc[...] = part if i == 0 else proj_acc[...] + part
        if i + 2 < n_wo:
            wo_copy(i + 2).start()

    def qkv_step(i):
        wq_copy(i).wait()
        part = dot(h_b[:, i * WQ_CHUNK:(i + 1) * WQ_CHUNK], wq_buf[i % 2])
        if i == n_wq - 1:
            qkv_out[...] = (qkv_acc[...] + part).astype(BF16)
        else:
            qkv_acc[...] = part if i == 0 else qkv_acc[...] + part
        if i + 2 < n_wq:
            wq_copy(i + 2).start()

    def prepare(b, rows, route, gate):
        lane = iota((TOK, N_EXP), 1)
        chosen = jnp.zeros((TOK, N_EXP), F32)
        gates = jnp.zeros((TOK, N_EXP), F32)
        for j in range(TOP_K):
            hit = route[:, j:j + 1] == lane
            chosen = jnp.where(hit, 1.0, chosen)
            gates = jnp.where(hit, gate[:, j:j + 1], gates)
        before = (iota((TOK, TOK), 0) > iota((TOK, TOK), 1)).astype(F32).astype(BF16)
        rank = dot(before, chosen.astype(BF16))
        rank = jnp.where(chosen > 0.5, rank, UNUSED).astype(BF16)
        for cls, (d1, d2, d3) in enumerate(CLASSES):
            w, s = WIDTHS[cls], STARTS[cls]
            b["ag"][cls][pos[d2], pos[d1], :, :w] = rows[:, s:s + w]
            b["ag"][cls][pos[d2], pos[d1], :, w:] = rank
            b["gg"][cls][pos[d1]] = gates

    def gather1(b):
        ops = []
        for cls, (d1, d2, d3) in enumerate(CLASSES):
            mine = b["ag"][cls].at[pos[d2], pos[d1]]
            for off in (2, 1, 3):
                ops.append(links.copy(mine, mine, along(d1, off)[1]))
        return ops

    def gather_gates(b):
        ops = []
        for cls, (d1, d2, d3) in enumerate(CLASSES):
            mine = b["gg"][cls].at[pos[d1]]
            for off in (2, 1, 3):
                ops.append(links.copy(mine, mine, along(d1, off)[1]))
        return ops

    def gather2(b, ops1):
        ops = []
        for cls, (d1, d2, d3) in enumerate(CLASSES):
            for op in ops1[3 * cls:3 * cls + 3]:
                op.wait_recv()
            mine = b["ag"][cls].at[pos[d2]]
            for off in (2, 1, 3):
                ops.append(links.copy(mine, mine, along(d2, off)[1]))
        return ops

    def exchange(b, ops2):
        ops = []
        n = CORES * 64
        slot = iota((n, 1), 0)
        src_mask = ((slot >> 2) & 15) == (iota((n, SIDE * SIDE * TOK), 1) >> 5)
        kth = (slot & 3).astype(F32)
        for cls, (d1, d2, d3) in enumerate(CLASSES):
            w = WIDTHS[cls]
            for op in ops2[3 * cls:3 * cls + 3]:
                op.wait_recv()
            ag, ps, pr = b["ag"][cls], b["ps"][cls], b["pr"][cls]
            ranks = ag[:, :, :, w:].reshape(SIDE * SIDE * TOK, N_EXP)
            for off in (2, 1, 3, 0):
                there, dev = along(d3, off)
                first = dev - core
                pick_exp = (iota((n, N_EXP), 1) == first + (slot >> 6)).astype(F32).astype(BF16)
                val = dot_nt(pick_exp, ranks)
                pick = jnp.where(src_mask & (val == kth), 1.0, 0.0).astype(BF16)
                got = dot(pick, ag[:, :, :, :w].reshape(SIDE * SIDE * TOK, w)).astype(BF16).reshape(CORES, SIDE, 16, w)
                ps[there] = got
                for flip in (0, 1):
                    there_core = core if flip == 0 else 1 - core
                    if off == 0 and flip == 0:
                        pr[there, core] = ps[there, core]
                        continue
                    ops.append(links.copy(ps.at[there, there_core], pr.at[pos[d3], core], first + there_core))
        return ops

    def experts(b, ops3):
        for op in ops3:
            op.wait_recv()
        pr = b["pr"]
        xbuf[:, :WIDTHS[0]] = pr[0][...].reshape(SLOTS, WIDTHS[0])
        for cls in (1, 2):
            s, w = STARTS[cls], WIDTHS[cls]
            xbuf[:, s:s + w] = dot(perms[cls - 1], pr[cls][...].reshape(SLOTS, w)).astype(BF16)

        @pl.loop(0, FF // 256)
        def _(i):
            cols = pl.ds(pl.multiple_of(i * 256, 256), 256)
            g = dot(xbuf[...], vg[:, cols])
            u = dot(xbuf[...], vu[:, cols])
            hbuf[:, cols] = (g * (1.0 / (1.0 + jnp.exp(-g))) * u).astype(BF16)

    def back1(b):
        ops = []
        r1 = b["r1"]
        for cls, (d1, d2, d3) in enumerate(CLASSES):
            w, s = WIDTHS[cls], STARTS[cls]
            if cls == 0:
                h = hbuf[...]
            else:
                h = dot(perms[cls + 1], hbuf[...]).astype(BF16)
            y = dot(h, vd[:, s:s + w]).astype(BF16)
            ps_y = b["pr"][cls]
            ps_y[...] = y.reshape(SIDE, CORES, SIDE, 16, w)
            for off in (2, 1, 3, 0):
                there, dev = along(d3, off)
                first = dev - core
                for flip in (0, 1):
                    there_core = core if flip == 0 else 1 - core
                    if off == 0 and flip == 0:
                        r1[cls][there * CORES + core] = ps_y[there, core]
                        continue
                    ops.append(links.copy(ps_y.at[there, there_core],
                                          r1[cls].at[pos[d3] * CORES + core], first + there_core))
        return ops

    def back2(b, ops1):
        ops = []
        for cls, (d1, d2, d3) in enumerate(CLASSES):
            for op in ops1[7 * cls:7 * cls + 7]:
                op.wait_recv()
            r1, r2 = b["r1"][cls], b["r2"][cls]
            for off in (2, 1, 3):
                there, dev = along(d2, off)
                ops.append(links.copy(r1.at[:, there], r2.at[pos[d2]], dev))
            r2[pos[d2]] = r1[:, pos[d2]]
        return ops

    def back3(b, ops2):
        ops = []
        slot = iota((SLOTS, 1), 0)
        col = iota((SIDE * TOK, SLOTS), 1)
        same = ((col >> 2) & 3) == (iota((SIDE * TOK, SLOTS), 0) >> 5)
        kth = (col & 3).astype(F32)
        for cls, (d1, d2, d3) in enumerate(CLASSES):
            w = WIDTHS[cls]
            owner = (pos[d1] * STRIDE[d1] + (slot >> 7) * STRIDE[d2] + ((slot >> 5) & 3) * STRIDE[d3] + ((slot >> 4) & 1))
            pick_exp = (iota((SLOTS, N_EXP), 1) == owner).astype(F32).astype(BF16)
            ranks = b["ag"][cls][pos[d2], :, :, w:].reshape(SIDE * TOK, N_EXP)
            g = b["gg"][cls][...].reshape(SIDE * TOK, N_EXP)
            g1 = g.astype(BF16)
            rest = g - g1.astype(F32)
            g2 = rest.astype(BF16)
            g3 = (rest - g2.astype(F32)).astype(BF16)
            keep = same & (dot_nt(ranks, pick_exp) == kth)
            for op in ops2[3 * cls:3 * cls + 3]:
                op.wait_recv()
            rows = b["r2"][cls][...].reshape(SLOTS, w)
            total = None
            for part in (g3, g2, g1):
                weight = jnp.where(keep, dot_nt(part, pick_exp), 0.0).astype(BF16)
                term = dot(weight, rows)
                total = term if total is None else total + term
            sm, r3 = b["sm"][cls], b["r3"][cls]
            sm[...] = total.reshape(SIDE, TOK, w)
            for off in (2, 1, 3):
                there, dev = along(d1, off)
                ops.append(links.copy(sm.at[there], r3.at[pos[d1]], dev))
            r3[pos[d1]] = sm[pos[d1]]
        return ops

    def finish(b, ops3, rows, out):
        for cls in range(3):
            w, s = WIDTHS[cls], STARTS[cls]
            for op in ops3[3 * cls:3 * cls + 3]:
                op.wait_recv()
            r3 = b["r3"][cls]
            total = (r3[0] + r3[1]) + (r3[2] + r3[3])
            out[:, s:s + w] = (rows[:, s:s + w].astype(F32) + total).astype(BF16)

    a, b = bufs
    prepare(a, x_a, route_a, gate_a)
    pl.semaphore_wait(barrier, len(peers))
    a1 = gather1(a)
    for i in range(4):
        proj_step(i)
    a2 = gather2(a, a1)
    for i in range(4, n_wo):
        proj_step(i)
    u_b[...] = (h_b[...].astype(F32) + proj_acc[...].astype(BF16).astype(F32)).astype(BF16)
    prepare(b, u_b, route_b, gate_b)
    b1 = gather1(b)
    perms[0] = reorder(0, 1)
    perms[1] = reorder(0, 2)
    perms[2] = reorder(1, 0)
    perms[3] = reorder(2, 0)
    b2 = gather2(b, b1)
    ag_gates = gather_gates(a)
    bg_gates = gather_gates(b)
    a3 = exchange(a, a2)
    for i in range(4):
        qkv_step(i)
    b3 = exchange(b, b2)
    for i in range(4, n_wq):
        qkv_step(i)
    for c in w_copies:
        c.wait()
    experts(a, a3)
    a4 = back1(a)
    experts(b, b3)
    b4 = back1(b)
    for op in ag_gates + bg_gates:
        op.wait_recv()
    a5 = back2(a, a4)
    b5 = back2(b, b4)
    a6 = back3(a, a5)
    b6 = back3(b, b5)
    finish(a, a6, x_a, out_a)
    finish(b, b6, u_b, out_b)
    links.drain()


def solution(mesh):
    def local_step(x_a, route_a, gate_a, h_b, attn_b, route_b, gate_b, w_qkv, w_o, w_gate, w_up, w_down):
        vmem = pl.BlockSpec(memory_space=pltpu.VMEM)
        hbm = pl.BlockSpec(memory_space=pl.ANY)
        scratch = []
        for _ in range(2):
            for shape, dtype in (
                (lambda w: (SIDE, SIDE, TOK, w + N_EXP), BF16),
                (lambda w: (SIDE, CORES, SIDE, 16, w), BF16),
                (lambda w: (SIDE, CORES, SIDE, 16, w), BF16),
                (lambda w: (SIDE * CORES, SIDE, 16, w), BF16),
                (lambda w: (SIDE, SIDE * CORES, 16, w), BF16),
                (lambda w: (SIDE, TOK, w), F32),
                (lambda w: (SIDE, TOK, w), F32),
                (lambda w: (SIDE, TOK, N_EXP), F32),
            ):
                scratch += [pltpu.VMEM(shape(w), dtype) for w in WIDTHS]
        scratch += [
            pltpu.VMEM((SLOTS, D), BF16),
            pltpu.VMEM((SLOTS, FF), BF16),
            pltpu.VMEM((4, SLOTS, SLOTS), BF16),
            pltpu.VMEM((TOK, D), F32),
            pltpu.VMEM((TOK, QKV), F32),
            pltpu.VMEM((TOK, D), BF16),
            pltpu.VMEM((D, FF), BF16),
            pltpu.VMEM((D, FF), BF16),
            pltpu.VMEM((FF, D), BF16),
            pltpu.VMEM((2, WO_CHUNK, D), BF16),
            pltpu.VMEM((2, WQ_CHUNK, QKV), BF16),
            pltpu.SemaphoreType.DMA((n_copies(),)),
            pltpu.SemaphoreType.DMA((n_copies(),)),
            pltpu.SemaphoreType.DMA((3,)),
            pltpu.SemaphoreType.DMA((2,)),
            pltpu.SemaphoreType.DMA((2,)),
        ]
        return pl.pallas_call(
            kernel,
            out_shape=(
                jax.ShapeDtypeStruct((TOK, D), BF16),
                jax.ShapeDtypeStruct((TOK, D), BF16),
                jax.ShapeDtypeStruct((TOK, QKV), BF16),
            ),
            in_specs=[vmem] * 7 + [hbm] * 5,
            out_specs=(vmem, vmem, vmem),
            scratch_shapes=scratch,
            name="moe_pair",
            compiler_params=pltpu.CompilerParams(
                collective_id=0, has_side_effects=True, vmem_limit_bytes=64 * 2**20 - 2**16),
        )(x_a, h_b, attn_b, route_a, route_b, gate_a, gate_b, w_qkv, w_o, w_gate, w_up, w_down)

    row_spec = P(("dp", "ep"), None)
    full_spec = P(None, None)
    expert_spec = P("ep", None, None)
    return jax.shard_map(
        local_step,
        mesh=mesh,
        in_specs=(row_spec,) * 7 + (full_spec, full_spec) + (expert_spec,) * 3,
        out_specs=(row_spec, row_spec, row_spec),
        check_vma=False,
    )
```

time: 173 us -> 118 us (0.68)
  Pallas kernels: 0 us -> 106 us
  matrix products: 55.7 us -> 0 us
  waiting for transfers between devices: 45.1 us -> 0 us
  starting transfers between devices: 28.5 us -> 0 us
  local copies, waits for them, and re-layouts: 36.5 us -> 10.3 us
  other arithmetic: 4.83 us -> 0 us
    pallas_call x0 -> x1, Pallas kernels: none -> 106 us  [local_step(): pl.pallas_call(kernel, out_shape=(jax.ShapeDtypeStruct((TOK, D), BF16), j...]
    dot_general x10 -> x0, matrix products: 55.7 us -> none  [the longest x2 16.6 us: expert_ffn(): jnp.einsum('erf,efd->erd', hidden, w_down, preferred_element_type=jnp.flo...]
    all_to_all x4 -> x0, waiting for transfers between devices: 45.1 us -> none  [the longest x2 24.7 us: moe_local(): recv_buf = lax.all_to_all(send_buf, 'ep', 1, 1, tiled=True)]
    all_to_all x4 -> x0, starting transfers between devices: 28.5 us -> none  [the longest x2 17.5 us: moe_local(): recv_buf = lax.all_to_all(send_buf, 'ep', 1, 1, tiled=True)]
    reshape x6 -> x0, local copies, waits for them, and re-layouts: 22.4 us -> none  [the longest x2 8.22 us: moe_local(): send_buf = send_buf.reshape(local_n, n_devs, capacity, model_dim)]
    unnamed x56 -> x7, local copies, waits for them, and re-layouts: 1.49 us -> 10.3 us
    another operation x6 -> x0, local copies, waits for them, and re-layouts: 7.98 us -> none
    slice x1 -> x0, local copies, waits for them, and re-layouts: 2.62 us -> none  [moe_local(): mixture = mixture + gate_vals[:, choice:choice + 1] * picked[:, choice]]
  transfers between devices with their start and end apart: 4 -> 0, of which waited for: 4 -> 0; matrix products, arithmetic and copies ran while one was open for 47% -> 0% of each run, Pallas kernels for 0% -> 0%
where the time goes in v1:
time: 118 us; the launch traced here: 116 us
  Pallas kernels  106 us (90%)
  local copies, waits for them, and re-layouts  10.3 us (9%)
    pallas_call x1, Pallas kernels, local_step(): pl.pallas_call(kernel, out_shape=(jax.ShapeDtypeStruct((TOK, D), BF16), j...  106 us
    unnamed x7, local copies, waits for them, and re-layouts  10.3 us

profile of v1, /device:TPU:0, one launch (start us, length us, event | category | flops | bytes accessed | tf_op | source)
XLA Modules:
  0.0 116.5 jit_solution(10592441652900981489)
XLA Ops:
  0.6 1.4 %copy.15.refs_3_ = s32[32,8]{1,0:T(8,128)} copy(s32[32,8]{0,1:T(8,128)} %param.13) | data formatting | bytes 2048 | tf_op args[1]
  2.0 1.4 %copy.17.refs_5_ = f32[32,8]{1,0:T(8,128)} copy(f32[32,8]{0,1:T(8,128)} %param.14) | data formatting | bytes 2048 | tf_op args[2]
  3.4 1.4 %copy.16.refs_4_ = s32[32,8]{1,0:T(8,128)} copy(s32[32,8]{0,1:T(8,128)} %param.17) | data formatting | bytes 2048 | tf_op args[5]
  4.7 1.4 %copy.18.refs_6_ = f32[32,8]{1,0:T(8,128)} copy(f32[32,8]{0,1:T(8,128)} %param.18) | data formatting | bytes 2048 | tf_op args[6]
  6.1 105.5 %moe_pair.1 = (bf16[32,2048]{1,0:T(8,128)(2,1)}, bf16[32,2048]{1,0:T(8,128)(2,1)}, bf16[32,5120]{1,0:T(8,128)(2,1)}) custom-call(bf16[32,2048]{1,0:T(8,128)(2,1)} %refs_0_.1, bf16[32,2048]{1,0:T(8,128)(2,1)} %refs_1_.1, bf16[32,4096]{1,0:T(8,128)(2,1)} %refs_2_.1, s32[32,8]{1,0:T(8,128)} %copy.15.refs_3_, s32[32,8]{1,0:T(8,128)} %copy.16.refs_4_, ...), custom_call_target="tpu_custom_call" | custom-call | tf_op jit(solution)/shard_map/moe_pair/pallas_call | solution.py:398
  111.6 1.6 %copy.22 = bf16[32,2048]{1,0:T(8,128)(2,1)} copy(bf16[32,2048]{1,0:T(8,128)(2,1)} %get-tuple-element.6) | data formatting | bytes 262144
  113.2 1.6 %copy.23 = bf16[32,2048]{1,0:T(8,128)(2,1)} copy(bf16[32,2048]{1,0:T(8,128)(2,1)} %get-tuple-element.7) | data formatting | bytes 262144
  114.8 1.7 %copy.24 = bf16[32,5120]{1,0:T(8,128)(2,1)} copy(bf16[32,5120]{1,0:T(8,128)(2,1)} %get-tuple-element.8) | data formatting | bytes 655360

commit v2 on v1

v2 whole, which is shorter than its diff:
```python
import jax
import jax.numpy as jnp
from jax import lax
from jax.experimental import pallas as pl
from jax.experimental.pallas import tpu as pltpu
from jax.sharding import PartitionSpec as P

MESH = pl.DeviceIdType.MESH
BF16 = jnp.bfloat16
F32 = jnp.float32

SIDE = 4
CORES = 2
TOK = 32
CAP = 4
TOP_K = 8
D = 2048
N_EXP = 128
FF = 768
ATT = 4096
QKV = 5120
SLOTS = N_EXP * CAP
CLASSES = ((0, 1, 2), (1, 2, 0), (2, 0, 1))
WIDTHS = ((768, 640, 640), (640, 768, 640))
STARTS = ((0, 768, 1408), (0, 640, 1408))
STRIDE = (32, 8, 2)
UNUSED = 8.0
WO_CHUNK = 512
WQ_CHUNK = 256
HALF = SLOTS // 2
COLUMN = SIDE * TOK


def iota(shape, dim):
    return lax.broadcasted_iota(jnp.int32, shape, dim)


def ones_where(cond):
    return jnp.where(cond, 1.0, 0.0).astype(BF16)


def dot(a, b):
    return jnp.dot(a, b, preferred_element_type=F32)


def dot_nt(a, b):
    return lax.dot_general(a, b, (((1,), (1,)), ((), ())), preferred_element_type=F32)


def reorder(to_cls, from_cls):
    row = iota((HALF, 1), 0)
    d1, d2, d3 = CLASSES[to_cls]
    coords = {d3: row >> 6, d2: (row >> 4) & 3, d1: (row >> 2) & 3}
    d1, d2, d3 = CLASSES[from_cls]
    want = (coords[d3] << 6) | (coords[d2] << 4) | (coords[d1] << 2) | (row & 3)
    return ones_where(iota((HALF, HALF), 1) == want)


class Links:
    def __init__(self, send, recv):
        self.send, self.recv, self.open = send, recv, []

    def copy(self, src, dst, device):
        i = len(self.open)
        op = pltpu.make_async_remote_copy(
            src_ref=src, dst_ref=dst, send_sem=self.send.at[i], recv_sem=self.recv.at[i],
            device_id={"ep": device}, device_id_type=MESH)
        op.start()
        self.open.append(op)
        return op

    def drain(self):
        for op in self.open:
            op.wait_send()


def arrived(ops):
    for op in ops:
        op.wait_recv()


N_COPIES = 18 + 2 * (9 + 12 + 84 + 21 + 36 + 9)


def kernel(*refs):
    it = iter(refs)
    take = lambda n: [next(it) for _ in range(n)]
    x_a, h_b, attn, route_a, route_b, gate_a, gate_b = take(7)
    w_qkv, w_o, w_gate, w_up, w_down = take(5)
    out_a, out_b, qkv_out = take(3)
    batches = []
    for m in range(2):
        b = {"m": m, "w": WIDTHS[m], "s": STARTS[m]}
        for name in ("ag", "ps", "pr", "r1", "r2", "sm", "r3"):
            b[name] = take(3)
        batches.append(b)
    meta, routes, gates = take(3), take(3), take(3)
    xbuf, hbuf, perms, proj_acc, qkv_acc, u_b = take(6)
    vg, vu, vd, wo_buf, wq_buf = take(5)
    send_sem, recv_sem, w_sem, wo_sem, wq_sem = take(5)

    me = lax.axis_index("ep")
    core = lax.rem(me, 2)
    pos = [lax.rem(me // 32, 4), lax.rem(me // 8, 4), lax.rem(me // 2, 4)]
    links = Links(send_sem, recv_sem)

    def along(dim, off):
        there = lax.rem(pos[dim] + off, 4)
        return there, me + (there - pos[dim]) * STRIDE[dim]

    peers = []
    for dim in range(3):
        for off in (1, 2, 3):
            _, dev = along(dim, off)
            peers += [dev, dev + 1 - 2 * core]
    peers.append(me + 1 - 2 * core)
    barrier = pltpu.get_barrier_semaphore()
    for dev in peers:
        pl.semaphore_signal(barrier, inc=1, device_id={"ep": dev}, device_id_type=MESH)

    w_copies = [pltpu.make_async_copy(src.at[0], dst, w_sem.at[i])
                for i, (src, dst) in enumerate(((w_gate, vg), (w_up, vu), (w_down, vd)))]
    n_wo, n_wq = ATT // WO_CHUNK, D // WQ_CHUNK

    def wo_copy(i):
        return pltpu.make_async_copy(w_o.at[pl.ds(i * WO_CHUNK, WO_CHUNK)], wo_buf.at[i % 2], wo_sem.at[i % 2])

    def wq_copy(i):
        return pltpu.make_async_copy(w_qkv.at[pl.ds(i * WQ_CHUNK, WQ_CHUNK)], wq_buf.at[i % 2], wq_sem.at[i % 2])

    wo_copy(0).start()
    wo_copy(1).start()
    for c in w_copies:
        c.start()
    wq_copy(0).start()
    wq_copy(1).start()

    def proj_step(i):
        wo_copy(i).wait()
        part = dot(attn[:, i * WO_CHUNK:(i + 1) * WO_CHUNK], wo_buf[i % 2])
        proj_acc[...] = part if i == 0 else proj_acc[...] + part
        if i + 2 < n_wo:
            wo_copy(i + 2).start()

    def qkv_step(i):
        wq_copy(i).wait()
        part = dot(h_b[:, i * WQ_CHUNK:(i + 1) * WQ_CHUNK], wq_buf[i % 2])
        if i == n_wq - 1:
            qkv_out[...] = (qkv_acc[...] + part).astype(BF16)
        else:
            qkv_acc[...] = part if i == 0 else qkv_acc[...] + part
        if i + 2 < n_wq:
            wq_copy(i + 2).start()

    earlier = ones_where((iota((COLUMN, COLUMN), 0) < iota((COLUMN, COLUMN), 1))
                         & (iota((COLUMN, COLUMN), 0) >> 5 == iota((COLUMN, COLUMN), 1) >> 5))

    def rank_of(route, expert):
        hit = route[0:1] == expert
        for j in range(1, TOP_K):
            hit = hit | (route[j:j + 1] == expert)
        rank = dot(ones_where(hit), earlier)
        return jnp.where(hit, rank, UNUSED)

    def write_meta():
        for cls, (d1, d2, d3) in enumerate(CLASSES):
            for i, (a, b) in enumerate(((route_a, route_b), (gate_a, gate_b))):
                meta[cls][pos[d1], i] = jnp.zeros((TOP_K, N_EXP), F32)
                meta[cls][pos[d1], i, :, 0:TOK] = a[...].astype(F32)
                meta[cls][pos[d1], i, :, TOK:2 * TOK] = b[...].astype(F32)

    def send_meta1():
        ops = []
        for cls, (d1, d2, d3) in enumerate(CLASSES):
            mine = meta[cls].at[pos[d1]]
            for off in (2, 1, 3):
                ops.append(links.copy(mine, mine, along(d1, off)[1]))
        return ops

    def send_meta2(ops1):
        lane = iota((TOP_K, COLUMN), 1) >> 5
        ops = []
        for cls, (d1, d2, d3) in enumerate(CLASSES):
            arrived(ops1[3 * cls:3 * cls + 3])
            for i, dst in ((0, routes[cls].at[pos[d2]]), (1, gates[cls])):
                for m in range(2):
                    packed = jnp.zeros((TOP_K, COLUMN), F32)
                    for v in range(SIDE):
                        shift = (TOK * (v - m)) % COLUMN
                        piece = meta[cls][v, i]
                        packed = jnp.where(lane == v, pltpu.roll(piece, shift, 1) if shift else piece, packed)
                    dst[m] = packed
            mine = routes[cls].at[pos[d2]]
            for off in (2, 1, 3):
                ops.append(links.copy(mine, mine, along(d2, off)[1]))
        return ops

    def gather1(b, rows):
        ops = []
        for cls, (d1, d2, d3) in enumerate(CLASSES):
            w, s = b["w"][cls], b["s"][cls]
            for off in (2, 1, 3):
                ops.append(links.copy(rows.at[:, s:s + w], b["ag"][cls].at[pos[d2], pos[d1]], along(d1, off)[1]))
        for cls, (d1, d2, d3) in enumerate(CLASSES):
            w, s = b["w"][cls], b["s"][cls]
            b["ag"][cls][pos[d2], pos[d1]] = rows[:, s:s + w]
        return ops

    def gather2(b, ops1):
        ops = []
        for cls, (d1, d2, d3) in enumerate(CLASSES):
            arrived(ops1[3 * cls:3 * cls + 3])
            mine = b["ag"][cls].at[pos[d2]]
            for off in (1, 3):
                ops.append(links.copy(mine, mine, along(d2, off)[1]))
        return ops

    def relay2(b, ops2):
        ops = []
        for cls, (d1, d2, d3) in enumerate(CLASSES):
            arrived(ops2[2 * cls:2 * cls + 2])
            for off, half in ((1, 0), (3, 2)):
                got = b["ag"][cls].at[along(d2, 4 - off)[0], half:half + 2]
                ops.append(links.copy(got, got, along(d2, off)[1]))
        return ops

    def pick(b, cls, off2):
        d1, d2, d3 = CLASSES[cls]
        w = b["w"][cls]
        block = along(d2, off2)[0]
        exp = iota((SIDE * CORES, 1), 0)
        exp = me - pos[d3] * STRIDE[d3] - core + (exp >> 1) * STRIDE[d3] + (exp & 1)
        rank = rank_of(routes[cls][block, b["m"]], exp.astype(F32))
        rank = jnp.concatenate([jnp.broadcast_to(rank[e:e + 1], (16, COLUMN)) for e in range(SIDE * CORES)], axis=0)
        slot = iota((COLUMN, 1), 0)
        mask = ((slot >> 2) & 3) == (iota((COLUMN, COLUMN), 1) >> 5)
        choice = ones_where(mask & (rank == (slot & 3).astype(F32)))
        got = dot(choice, b["ag"][cls][block].reshape(COLUMN, w)).astype(BF16)
        ps, pr = b["ps"][cls], b["pr"][cls]
        ps[block] = got.reshape(SIDE, CORES, 16, w)
        ops = []
        for off in (2, 1, 3, 0):
            there, dev = along(d3, off)
            first = dev - core
            for flip in (0, 1):
                there_core = core if flip == 0 else 1 - core
                if off == 0 and flip == 0:
                    pr[there, core, block] = ps[block, there, core]
                    continue
                ops.append(links.copy(ps.at[block, there, there_core], pr.at[pos[d3], core, block], first + there_core))
        return ops

    def experts(b, ops3):
        arrived(ops3)
        pr = b["pr"]
        for cls in range(3):
            s, w = b["s"][cls], b["w"][cls]
            for c in range(CORES):
                rows = pr[cls][:, c].reshape(HALF, w)
                if cls:
                    rows = dot(perms[cls - 1], rows).astype(BF16)
                xbuf[:, c, :, s:s + w] = rows.reshape(SIDE, 64, w)

        @pl.loop(0, FF // 256)
        def _(i):
            cols = pl.ds(pl.multiple_of(i * 256, 256), 256)
            x = xbuf[...].reshape(SLOTS, D)
            g = dot(x, vg[:, cols])
            u = dot(x, vu[:, cols])
            h = (g * (1.0 / (1.0 + jnp.exp(-g))) * u).astype(BF16)
            hbuf[:, :, :, cols] = h.reshape(SIDE, CORES, 64, 256)

    def back1(b):
        ops = []
        for cls, (d1, d2, d3) in enumerate(CLASSES):
            w, s = b["w"][cls], b["s"][cls]
            r1, y = b["r1"][cls], b["pr"][cls]
            for c in range(CORES):
                h = hbuf[:, c].reshape(HALF, FF)
                if cls:
                    h = dot(perms[cls + 1], h).astype(BF16)
                y[:, c] = dot(h, vd[:, s:s + w]).astype(BF16).reshape(SIDE, SIDE, 16, w)
            for off in (2, 1, 3, 0):
                there, dev = along(d3, off)
                first = dev - core
                for flip in (0, 1):
                    there_core = core if flip == 0 else 1 - core
                    if off == 0 and flip == 0:
                        r1[there, core] = y[there, core]
                        continue
                    ops.append(links.copy(y.at[there, there_core], r1.at[pos[d3], core], first + there_core))
        return ops

    def back2(b, ops1):
        ops = []
        for cls, (d1, d2, d3) in enumerate(CLASSES):
            r1, r2 = b["r1"][cls], b["r2"][cls]
            mine = ops1[7 * cls:7 * cls + 7]
            for off, got in ((0, mine[6:7]), (3, mine[2:4]), (1, mine[4:6]), (2, mine[0:2])):
                arrived(got)
                chip = along(d3, off)[0]
                for to in (2, 1, 3):
                    there, dev = along(d2, to)
                    ops.append(links.copy(r1.at[chip, :, there], r2.at[pos[d2], chip], dev))
                r2[pos[d2], chip] = r1[chip, :, pos[d2]]
        return ops

    def weights(b, cls):
        d1, d2, d3 = CLASSES[cls]
        m = b["m"]
        route = routes[cls][pos[d2], m]
        gate = gates[cls][m]
        exp = iota((N_EXP, 1), 0).astype(F32)
        rank = rank_of(route, exp)
        value = jnp.zeros((N_EXP, COLUMN), F32)
        for j in range(TOP_K):
            value = jnp.where(route[j:j + 1] == exp, gate[j:j + 1], value)
        rank, value = rank.T.astype(BF16), value.T
        slot = iota((SLOTS, 1), 0)
        owner = pos[d1] * STRIDE[d1] + (slot >> 7) * STRIDE[d2] + ((slot >> 5) & 3) * STRIDE[d3] + ((slot >> 4) & 1)
        onehot = ones_where(iota((SLOTS, N_EXP), 1) == owner)
        col = iota((COLUMN, SLOTS), 1)
        keep = ((col >> 2) & 3) == (iota((COLUMN, SLOTS), 0) >> 5)
        keep = keep & (dot_nt(rank, onehot) == (col & 3).astype(F32))
        part1 = value.astype(BF16)
        rest = value - part1.astype(F32)
        part2 = rest.astype(BF16)
        part3 = (rest - part2.astype(F32)).astype(BF16)
        return jnp.concatenate(
            [jnp.where(keep, dot_nt(part, onehot), 0.0).astype(BF16) for part in (part3, part2, part1)], axis=0)

    def back3(b, ops2):
        ops = []
        for cls, (d1, d2, d3) in enumerate(CLASSES):
            w = b["w"][cls]
            weight = weights(b, cls)
            arrived(ops2[12 * cls:12 * cls + 12])
            terms = dot(weight, b["r2"][cls][...].reshape(SLOTS, w)).reshape(3, COLUMN, w)
            sm, r3 = b["sm"][cls], b["r3"][cls]
            sm[...] = ((terms[0] + terms[1]) + terms[2]).reshape(SIDE, TOK, w)
            for off in (2, 1, 3):
                there, dev = along(d1, off)
                ops.append(links.copy(sm.at[there], r3.at[pos[d1]], dev))
            r3[pos[d1]] = sm[pos[d1]]
        return ops

    def finish(b, ops3, rows, out):
        for cls in range(3):
            w, s = b["w"][cls], b["s"][cls]
            arrived(ops3[3 * cls:3 * cls + 3])
            r3 = b["r3"][cls]
            total = (r3[0] + r3[1]) + (r3[2] + r3[3])
            out[:, s:s + w] = (rows[:, s:s + w].astype(F32) + total).astype(BF16)

    a, b = batches
    write_meta()
    pl.semaphore_wait(barrier, len(peers))
    a1 = gather1(a, x_a)
    m1 = send_meta1()
    proj_step(0)
    proj_step(1)
    a2 = gather2(a, a1)
    m2 = send_meta2(m1)
    proj_step(2)
    a3 = []
    for cls in range(3):
        a3 += pick(a, cls, 0)
    proj_step(3)
    proj_step(4)
    ar = relay2(a, a2)
    proj_step(5)
    arrived(m2)
    for cls in range(3):
        a3 += pick(a, cls, 1)
    proj_step(6)
    for cls in range(3):
        a3 += pick(a, cls, 3)
    proj_step(7)
    u_b[...] = (h_b[...].astype(F32) + proj_acc[...].astype(BF16).astype(F32)).astype(BF16)
    b1 = gather1(b, u_b)
    for cls in range(3):
        arrived(ar[2 * cls:2 * cls + 2])
        a3 += pick(a, cls, 2)
    b2 = gather2(b, b1)
    perms[0] = reorder(0, 1)
    perms[1] = reorder(0, 2)
    perms[2] = reorder(1, 0)
    perms[3] = reorder(2, 0)
    b3 = []
    for cls in range(3):
        b3 += pick(b, cls, 0)
    qkv_step(0)
    br = relay2(b, b2)
    for cls in range(3):
        b3 += pick(b, cls, 1)
        b3 += pick(b, cls, 3)
    qkv_step(1)
    for cls in range(3):
        arrived(br[2 * cls:2 * cls + 2])
        b3 += pick(b, cls, 2)
    for c in w_copies:
        c.wait()
    experts(a, a3)
    a4 = back1(a)
    experts(b, b3)
    b4 = back1(b)
    a5 = back2(a, a4)
    for i in range(2, 5):
        qkv_step(i)
    b5 = back2(b, b4)
    for i in range(5, n_wq):
        qkv_step(i)
    a6 = back3(a, a5)
    b6 = back3(b, b5)
    finish(a, a6, x_a, out_a)
    finish(b, b6, u_b, out_b)
    links.drain()


def deliver(*refs):
    n = (len(refs) - 1) // 2
    ops = [pltpu.make_async_copy(refs[i], refs[n + i], refs[-1].at[i]) for i in range(n)]
    for op in ops:
        op.start()
    for op in ops:
        op.wait()


def solution(mesh):
    def local_step(x_a, route_a, gate_a, h_b, attn_b, route_b, gate_b, w_qkv, w_o, w_gate, w_up, w_down):
        vmem = pl.BlockSpec(memory_space=pltpu.VMEM)
        hbm = pl.BlockSpec(memory_space=pl.ANY)
        scratch = []
        for m in range(2):
            for shape, dtype in (
                (lambda w: (SIDE, SIDE, TOK, w), BF16),
                (lambda w: (SIDE, SIDE, CORES, 16, w), BF16),
                (lambda w: (SIDE, CORES, SIDE, 16, w), BF16),
                (lambda w: (SIDE, CORES, SIDE, 16, w), BF16),
                (lambda w: (SIDE, SIDE, CORES, 16, w), BF16),
                (lambda w: (SIDE, TOK, w), F32),
                (lambda w: (SIDE, TOK, w), F32),
            ):
                scratch += [pltpu.VMEM(shape(w), dtype) for w in WIDTHS[m]]
        scratch += [pltpu.VMEM((SIDE, 2, TOP_K, COLUMN), F32)] * 3
        scratch += [pltpu.VMEM((SIDE, 2, TOP_K, COLUMN), F32)] * 3
        scratch += [pltpu.VMEM((2, TOP_K, COLUMN), F32)] * 3
        scratch += [
            pltpu.VMEM((SIDE, CORES, 64, D), BF16),
            pltpu.VMEM((SIDE, CORES, 64, FF), BF16),
            pltpu.VMEM((4, HALF, HALF), BF16),
            pltpu.VMEM((TOK, D), F32),
            pltpu.VMEM((TOK, QKV), F32),
            pltpu.VMEM((TOK, D), BF16),
            pltpu.VMEM((D, FF), BF16),
            pltpu.VMEM((D, FF), BF16),
            pltpu.VMEM((FF, D), BF16),
            pltpu.VMEM((2, WO_CHUNK, D), BF16),
            pltpu.VMEM((2, WQ_CHUNK, QKV), BF16),
            pltpu.SemaphoreType.DMA((N_COPIES,)),
            pltpu.SemaphoreType.DMA((N_COPIES,)),
            pltpu.SemaphoreType.DMA((3,)),
            pltpu.SemaphoreType.DMA((2,)),
            pltpu.SemaphoreType.DMA((2,)),
        ]
        outs = tuple(jax.ShapeDtypeStruct((TOK, n), BF16) for n in (D, D, QKV))
        results = pl.pallas_call(
            kernel,
            out_shape=outs,
            in_specs=[vmem] * 7 + [hbm] * 5,
            out_specs=(vmem,) * 3,
            scratch_shapes=scratch,
            name="moe_pair",
            compiler_params=pltpu.CompilerParams(
                collective_id=0, has_side_effects=True, vmem_limit_bytes=64 * 2**20 - 2**16),
        )(x_a, h_b, attn_b, route_a.T, route_b.T, gate_a.T, gate_b.T, w_qkv, w_o, w_gate, w_up, w_down)
        return pl.pallas_call(
            deliver,
            out_shape=outs,
            in_specs=[hbm] * 3,
            out_specs=(vmem,) * 3,
            scratch_shapes=[pltpu.SemaphoreType.DMA((3,))],
            name="deliver",
        )(*results)

    row_spec = P(("dp", "ep"), None)
    full_spec = P(None, None)
    expert_spec = P("ep", None, None)
    return jax.shard_map(
        local_step,
        mesh=mesh,
        in_specs=(row_spec,) * 7 + (full_spec, full_spec) + (expert_spec,) * 3,
        out_specs=(row_spec, row_spec, row_spec),
        check_vma=False,
    )
```

time: 118 us -> 102 us (0.86); the launches traced: 116 us -> 102 us
  local copies, waits for them, and re-layouts: 10.3 us -> 0 us
  Pallas kernels: 106 us -> 101 us
    unnamed x7 -> x0, local copies, waits for them, and re-layouts: 10.3 us -> none
    pallas_call x1 -> x2, Pallas kernels: 106 us -> 101 us  [the longest x1 99.2 us: local_step(): pl.pallas_call(kernel, out_shape=outs, in_specs=[vmem] * 7 + [hbm] * 5, o...]
where the time goes in v2:
time: 102 us
  Pallas kernels  101 us (99%)
    pallas_call x1, Pallas kernels, local_step(): pl.pallas_call(kernel, out_shape=outs, in_specs=[vmem] * 7 + [hbm] * 5, o...  99.2 us

profile of v2, /device:TPU:0, one launch (start us, length us, event | category | flops | bytes accessed | tf_op | source)
XLA Modules:
  0.0 101.9 jit_solution(16912638841948603968)
XLA Ops:
  0.6 99.2 %moe_pair.1 = (bf16[32,2048]{1,0:T(8,128)(2,1)}, bf16[32,2048]{1,0:T(8,128)(2,1)}, bf16[32,5120]{1,0:T(8,128)(2,1)}) custom-call(bf16[32,2048]{1,0:T(8,128)(2,1)} %refs_0_.1, bf16[32,2048]{1,0:T(8,128)(2,1)} %refs_1_.1, bf16[32,4096]{1,0:T(8,128)(2,1)} %refs_2_.1, s32[8,32]{1,0:T(8,128)} %bitcast.4, s32[8,32]{1,0:T(8,128)} %bitcast.5, f32[8,32]{1,0:T(8,128)} %bitcast.6, ...), custom_call_target="tpu_custom_call" | custom-call | tf_op jit(solution)/shard_map/moe_pair/pallas_call | solution.py:467
  99.8 1.9 %deliver.1 = (bf16[32,2048]{1,0:T(8,128)(2,1)}, bf16[32,2048]{1,0:T(8,128)(2,1)}, bf16[32,5120]{1,0:T(8,128)(2,1)}) custom-call(bf16[32,2048]{1,0:T(8,128)(2,1)} %get-tuple-element.6.refs_0_, bf16[32,2048]{1,0:T(8,128)(2,1)} %get-tuple-element.7.refs_1_, bf16[32,5120]{1,0:T(8,128)(2,1)} %get-tuple-element.8.refs_2_), custom_call_target="tpu_custom_call" | custom-call | tf_op jit(solution)/shard_map/deliver/pallas_call | solution.py:477

commit v3 on v2

--- a/solution.py
+++ b/solution.py
@@ -57,29 +57,29 @@
 
 
 class Links:
-    def __init__(self, send, recv):
-        self.send, self.recv, self.open = send, recv, []
-
-    def copy(self, src, dst, device):
-        i = len(self.open)
-        op = pltpu.make_async_remote_copy(
-            src_ref=src, dst_ref=dst, send_sem=self.send.at[i], recv_sem=self.recv.at[i],
+    def __init__(self, send, recv, other):
+        self.send, self.recv, self.other, self.sends, self.recvs = send, recv, other, {}, {}
+
+    def _op(self, src, dst, device, phase, group):
+        i = self.sends.setdefault(phase, len(self.sends))
+        j = self.recvs.setdefault(group, len(self.recvs))
+        return pltpu.make_async_remote_copy(
+            src_ref=src, dst_ref=dst, send_sem=self.send.at[i], recv_sem=self.recv.at[j],
             device_id={"ep": device}, device_id_type=MESH)
-        op.start()
-        self.open.append(op)
-        return op
-
-    def drain(self):
-        for op in self.open:
-            op.wait_send()
-
-
-def arrived(ops):
-    for op in ops:
-        op.wait_recv()
-
-
-N_COPIES = 18 + 2 * (9 + 12 + 84 + 21 + 36 + 9)
+
+    def copy(self, src, dst, device, phase, *rest):
+        self._op(src, dst, device, phase, phase + rest).start()
+
+    def arrived(self, like, phase, *rest):
+        self._op(like, like, self.other, phase, phase + rest).wait_recv()
+
+    def sent(self, like, phase):
+        self._op(like, like, self.other, phase, next(g for g in self.recvs if g[:len(phase)] == phase)).wait_send()
+
+
+N_PHASES = 6 + 2 * 21
+N_GROUPS = 6 + 2 * (3 + 3 + 3 + 3 + 24 + 6 + 6)
+FIRST = 384
 
 
 def kernel(*refs):
@@ -95,14 +95,14 @@
             b[name] = take(3)
         batches.append(b)
     meta, routes, gates = take(3), take(3), take(3)
-    xbuf, hbuf, perms, proj_acc, qkv_acc, u_b = take(6)
+    xbuf, hbuf, hperm, wts, perms, proj_acc, qkv_acc, u_b = take(8)
     vg, vu, vd, wo_buf, wq_buf = take(5)
     send_sem, recv_sem, w_sem, wo_sem, wq_sem = take(5)
 
     me = lax.axis_index("ep")
     core = lax.rem(me, 2)
     pos = [lax.rem(me // 32, 4), lax.rem(me // 8, 4), lax.rem(me // 2, 4)]
-    links = Links(send_sem, recv_sem)
+    links = Links(send_sem, recv_sem, me + 1 - 2 * core)
 
     def along(dim, off):
         there = lax.rem(pos[dim] + off, 4)
@@ -170,18 +170,15 @@
                 meta[cls][pos[d1], i, :, TOK:2 * TOK] = b[...].astype(F32)
 
     def send_meta1():
-        ops = []
         for cls, (d1, d2, d3) in enumerate(CLASSES):
             mine = meta[cls].at[pos[d1]]
             for off in (2, 1, 3):
-                ops.append(links.copy(mine, mine, along(d1, off)[1]))
-        return ops
-
-    def send_meta2(ops1):
+                links.copy(mine, mine, along(d1, off)[1], ("meta1", cls))
+
+    def send_meta2():
         lane = iota((TOP_K, COLUMN), 1) >> 5
-        ops = []
-        for cls, (d1, d2, d3) in enumerate(CLASSES):
-            arrived(ops1[3 * cls:3 * cls + 3])
+        for cls, (d1, d2, d3) in enumerate(CLASSES):
+            links.arrived(meta[cls].at[0:3], ("meta1", cls))
             for i, dst in ((0, routes[cls].at[pos[d2]]), (1, gates[cls])):
                 for m in range(2):
                     packed = jnp.zeros((TOP_K, COLUMN), F32)
@@ -192,37 +189,36 @@
                     dst[m] = packed
             mine = routes[cls].at[pos[d2]]
             for off in (2, 1, 3):
-                ops.append(links.copy(mine, mine, along(d2, off)[1]))
-        return ops
+                links.copy(mine, mine, along(d2, off)[1], ("meta2", cls))
 
     def gather1(b, rows):
-        ops = []
         for cls, (d1, d2, d3) in enumerate(CLASSES):
             w, s = b["w"][cls], b["s"][cls]
             for off in (2, 1, 3):
-                ops.append(links.copy(rows.at[:, s:s + w], b["ag"][cls].at[pos[d2], pos[d1]], along(d1, off)[1]))
+                links.copy(rows.at[:, s:s + w], b["ag"][cls].at[pos[d2], pos[d1]], along(d1, off)[1],
+                           ("gather1", b["m"], cls))
         for cls, (d1, d2, d3) in enumerate(CLASSES):
             w, s = b["w"][cls], b["s"][cls]
             b["ag"][cls][pos[d2], pos[d1]] = rows[:, s:s + w]
-        return ops
-
-    def gather2(b, ops1):
-        ops = []
-        for cls, (d1, d2, d3) in enumerate(CLASSES):
-            arrived(ops1[3 * cls:3 * cls + 3])
-            mine = b["ag"][cls].at[pos[d2]]
+
+    def gather2(b):
+        for cls, (d1, d2, d3) in enumerate(CLASSES):
+            ag = b["ag"][cls]
+            links.arrived(ag.at[0, 0:3], ("gather1", b["m"], cls))
+            mine = ag.at[pos[d2]]
             for off in (1, 3):
-                ops.append(links.copy(mine, mine, along(d2, off)[1]))
-        return ops
-
-    def relay2(b, ops2):
-        ops = []
-        for cls, (d1, d2, d3) in enumerate(CLASSES):
-            arrived(ops2[2 * cls:2 * cls + 2])
+                links.copy(mine, mine, along(d2, off)[1], ("gather2", b["m"], cls))
+
+    def relay2(b):
+        for cls, (d1, d2, d3) in enumerate(CLASSES):
+            ag = b["ag"][cls]
+            links.arrived(ag.at[0:2], ("gather2", b["m"], cls))
             for off, half in ((1, 0), (3, 2)):
-                got = b["ag"][cls].at[along(d2, 4 - off)[0], half:half + 2]
-                ops.append(links.copy(got, got, along(d2, off)[1]))
-        return ops
+                got = ag.at[along(d2, 4 - off)[0], half:half + 2]
+                links.copy(got, got, along(d2, off)[1], ("relay2", b["m"], cls))
+
+    def relayed(b, cls):
+        links.arrived(b["ag"][cls].at[0], ("relay2", b["m"], cls))
 
     def pick(b, cls, off2):
         d1, d2, d3 = CLASSES[cls]
@@ -238,25 +234,24 @@
         got = dot(choice, b["ag"][cls][block].reshape(COLUMN, w)).astype(BF16)
         ps, pr = b["ps"][cls], b["pr"][cls]
         ps[block] = got.reshape(SIDE, CORES, 16, w)
-        ops = []
         for off in (2, 1, 3, 0):
             there, dev = along(d3, off)
             first = dev - core
             for flip in (0, 1):
                 there_core = core if flip == 0 else 1 - core
                 if off == 0 and flip == 0:
-                    pr[there, core, block] = ps[block, there, core]
+                    pr[CORES * there + core, block] = ps[block, there, core]
                     continue
-                ops.append(links.copy(ps.at[block, there, there_core], pr.at[pos[d3], core, block], first + there_core))
-        return ops
-
-    def experts(b, ops3):
-        arrived(ops3)
-        pr = b["pr"]
+                links.copy(ps.at[block, there, there_core], pr.at[CORES * pos[d3] + core, block], first + there_core,
+                           ("pick", b["m"], cls))
+
+    def experts(b):
         for cls in range(3):
             s, w = b["s"][cls], b["w"][cls]
+            pr = b["pr"][cls]
+            links.arrived(pr.at[0:7], ("pick", b["m"], cls))
             for c in range(CORES):
-                rows = pr[cls][:, c].reshape(HALF, w)
+                rows = jnp.concatenate([pr[CORES * v + c].reshape(64, w) for v in range(SIDE)], axis=0)
                 if cls:
                     rows = dot(perms[cls - 1], rows).astype(BF16)
                 xbuf[:, c, :, s:s + w] = rows.reshape(SIDE, 64, w)
@@ -270,40 +265,49 @@
             h = (g * (1.0 / (1.0 + jnp.exp(-g))) * u).astype(BF16)
             hbuf[:, :, :, cols] = h.reshape(SIDE, CORES, 64, 256)
 
-    def back1(b):
-        ops = []
-        for cls, (d1, d2, d3) in enumerate(CLASSES):
-            w, s = b["w"][cls], b["s"][cls]
+    def lanes(b, cls, part):
+        return (0, FIRST) if part == 0 else (FIRST, b["w"][cls])
+
+    def align(b):
+        for cls in (1, 2):
+            for c in range(CORES):
+                hperm[cls - 1, c] = dot(perms[cls + 1], hbuf[:, c].reshape(HALF, FF)).astype(BF16)
+
+    def back1(b, part):
+        for cls, (d1, d2, d3) in enumerate(CLASSES):
+            s = b["s"][cls]
+            lo, hi = lanes(b, cls, part)
             r1, y = b["r1"][cls], b["pr"][cls]
             for c in range(CORES):
-                h = hbuf[:, c].reshape(HALF, FF)
-                if cls:
-                    h = dot(perms[cls + 1], h).astype(BF16)
-                y[:, c] = dot(h, vd[:, s:s + w]).astype(BF16).reshape(SIDE, SIDE, 16, w)
+                h = hperm[cls - 1, c] if cls else hbuf[:, c].reshape(HALF, FF)
+                out = dot(h, vd[:, s + lo:s + hi]).astype(BF16).reshape(SIDE, SIDE, 16, hi - lo)
+                for v in range(SIDE):
+                    y[CORES * v + c, :, :, lo:hi] = out[v]
             for off in (2, 1, 3, 0):
                 there, dev = along(d3, off)
                 first = dev - core
                 for flip in (0, 1):
                     there_core = core if flip == 0 else 1 - core
+                    mine = y.at[CORES * there + there_core, :, :, lo:hi]
                     if off == 0 and flip == 0:
-                        r1[there, core] = y[there, core]
+                        r1[there, core, :, :, lo:hi] = mine[...]
                         continue
-                    ops.append(links.copy(y.at[there, there_core], r1.at[pos[d3], core], first + there_core))
-        return ops
-
-    def back2(b, ops1):
-        ops = []
+                    links.copy(mine, r1.at[pos[d3], core, :, :, lo:hi], first + there_core,
+                               ("back1", b["m"], cls), part, off)
+
+    def back2(b, part):
         for cls, (d1, d2, d3) in enumerate(CLASSES):
             r1, r2 = b["r1"][cls], b["r2"][cls]
-            mine = ops1[7 * cls:7 * cls + 7]
-            for off, got in ((0, mine[6:7]), (3, mine[2:4]), (1, mine[4:6]), (2, mine[0:2])):
-                arrived(got)
-                chip = along(d3, off)[0]
+            lo, hi = lanes(b, cls, part)
+            for off in (0, 1, 3, 2):
+                chip = along(d3, (4 - off) % 4)[0]
+                like = r1.at[0, :, :, :, lo:hi] if off else r1.at[0, 0, :, :, lo:hi]
+                links.arrived(like, ("back1", b["m"], cls), part, off)
                 for to in (2, 1, 3):
                     there, dev = along(d2, to)
-                    ops.append(links.copy(r1.at[chip, :, there], r2.at[pos[d2], chip], dev))
-                r2[pos[d2], chip] = r1[chip, :, pos[d2]]
-        return ops
+                    links.copy(r1.at[chip, :, there, :, lo:hi], r2.at[pos[d2], chip, :, :, lo:hi], dev,
+                               ("back2", b["m"], cls), part)
+                r2[pos[d2], chip, :, :, lo:hi] = r1[chip, :, pos[d2], :, lo:hi]
 
     def weights(b, cls):
         d1, d2, d3 = CLASSES[cls]
@@ -329,92 +333,119 @@
         return jnp.concatenate(
             [jnp.where(keep, dot_nt(part, onehot), 0.0).astype(BF16) for part in (part3, part2, part1)], axis=0)
 
-    def back3(b, ops2):
-        ops = []
-        for cls, (d1, d2, d3) in enumerate(CLASSES):
-            w = b["w"][cls]
-            weight = weights(b, cls)
-            arrived(ops2[12 * cls:12 * cls + 12])
-            terms = dot(weight, b["r2"][cls][...].reshape(SLOTS, w)).reshape(3, COLUMN, w)
+    def weigh(b):
+        for cls in range(3):
+            wts[cls] = weights(b, cls)
+
+    def back3(b, part):
+        for cls, (d1, d2, d3) in enumerate(CLASSES):
+            lo, hi = lanes(b, cls, part)
+            links.arrived(b["r2"][cls].at[0:3, :, :, :, lo:hi], ("back2", b["m"], cls), part)
+            rows = b["r2"][cls][:, :, :, :, lo:hi].reshape(SLOTS, hi - lo)
+            terms = dot(wts[cls], rows).reshape(3, COLUMN, hi - lo)
             sm, r3 = b["sm"][cls], b["r3"][cls]
-            sm[...] = ((terms[0] + terms[1]) + terms[2]).reshape(SIDE, TOK, w)
+            sm[:, :, lo:hi] = ((terms[0] + terms[1]) + terms[2]).reshape(SIDE, TOK, hi - lo)
             for off in (2, 1, 3):
                 there, dev = along(d1, off)
-                ops.append(links.copy(sm.at[there], r3.at[pos[d1]], dev))
-            r3[pos[d1]] = sm[pos[d1]]
-        return ops
-
-    def finish(b, ops3, rows, out):
+                links.copy(sm.at[there, :, lo:hi], r3.at[pos[d1], :, lo:hi], dev, ("back3", b["m"], cls), part)
+            r3[pos[d1], :, lo:hi] = sm[pos[d1], :, lo:hi]
+
+    def finish(b, part, rows, out):
         for cls in range(3):
-            w, s = b["w"][cls], b["s"][cls]
-            arrived(ops3[3 * cls:3 * cls + 3])
+            s = b["s"][cls]
+            lo, hi = lanes(b, cls, part)
             r3 = b["r3"][cls]
-            total = (r3[0] + r3[1]) + (r3[2] + r3[3])
-            out[:, s:s + w] = (rows[:, s:s + w].astype(F32) + total).astype(BF16)
+            links.arrived(r3.at[0:3, :, lo:hi], ("back3", b["m"], cls), part)
+            total = (r3[0, :, lo:hi] + r3[1, :, lo:hi]) + (r3[2, :, lo:hi] + r3[3, :, lo:hi])
+            out[:, s + lo:s + hi] = (rows[:, s + lo:s + hi].astype(F32) + total).astype(BF16)
+
+    def drain(b, *names):
+        for cls in range(3):
+            likes = {"gather1": b["ag"][cls].at[0, 0:3], "gather2": b["ag"][cls].at[0:2], "relay2": b["ag"][cls].at[0],
+                     "pick": b["pr"][cls].at[0:7], "back1": b["pr"][cls].at[0:7], "back2": b["r2"][cls].at[0:3],
+                     "back3": b["r3"][cls].at[0:3]}
+            for name in names:
+                links.sent(likes[name], (name, b["m"], cls))
 
     a, b = batches
     write_meta()
     pl.semaphore_wait(barrier, len(peers))
-    a1 = gather1(a, x_a)
-    m1 = send_meta1()
+    gather1(a, x_a)
+    send_meta1()
     proj_step(0)
     proj_step(1)
-    a2 = gather2(a, a1)
-    m2 = send_meta2(m1)
+    gather2(a)
+    send_meta2()
     proj_step(2)
-    a3 = []
-    for cls in range(3):
-        a3 += pick(a, cls, 0)
+    for cls in range(3):
+        pick(a, cls, 0)
     proj_step(3)
     proj_step(4)
-    ar = relay2(a, a2)
+    relay2(a)
     proj_step(5)
-    arrived(m2)
-    for cls in range(3):
-        a3 += pick(a, cls, 1)
+    for cls in range(3):
+        links.arrived(routes[cls].at[0:3], ("meta2", cls))
+        pick(a, cls, 1)
     proj_step(6)
     for cls in range(3):
-        a3 += pick(a, cls, 3)
+        pick(a, cls, 3)
     proj_step(7)
     u_b[...] = (h_b[...].astype(F32) + proj_acc[...].astype(BF16).astype(F32)).astype(BF16)
-    b1 = gather1(b, u_b)
-    for cls in range(3):
-        arrived(ar[2 * cls:2 * cls + 2])
-        a3 += pick(a, cls, 2)
-    b2 = gather2(b, b1)
+    gather1(b, u_b)
+    for cls in range(3):
+        relayed(a, cls)
+        pick(a, cls, 2)
+    gather2(b)
     perms[0] = reorder(0, 1)
     perms[1] = reorder(0, 2)
     perms[2] = reorder(1, 0)
     perms[3] = reorder(2, 0)
-    b3 = []
-    for cls in range(3):
-        b3 += pick(b, cls, 0)
+    for cls in range(3):
+        pick(b, cls, 0)
     qkv_step(0)
-    br = relay2(b, b2)
-    for cls in range(3):
-        b3 += pick(b, cls, 1)
-        b3 += pick(b, cls, 3)
+    relay2(b)
+    for cls in range(3):
+        pick(b, cls, 1)
+        pick(b, cls, 3)
     qkv_step(1)
     for cls in range(3):
-        arrived(br[2 * cls:2 * cls + 2])
-        b3 += pick(b, cls, 2)
+        relayed(b, cls)
+        pick(b, cls, 2)
     for c in w_copies:
         c.wait()
-    experts(a, a3)
-    a4 = back1(a)
-    experts(b, b3)
-    b4 = back1(b)
-    a5 = back2(a, a4)
-    for i in range(2, 5):
+    experts(a)
+    align(a)
+    back1(a, 0)
+    back1(a, 1)
+    experts(b)
+    back2(a, 0)
+    align(b)
+    back1(b, 0)
+    back2(a, 1)
+    back1(b, 1)
+    weigh(a)
+    qkv_step(2)
+    back3(a, 0)
+    back2(b, 0)
+    qkv_step(3)
+    back3(a, 1)
+    back2(b, 1)
+    weigh(b)
+    for i in range(4, n_wq):
         qkv_step(i)
-    b5 = back2(b, b4)
-    for i in range(5, n_wq):
-        qkv_step(i)
-    a6 = back3(a, a5)
-    b6 = back3(b, b5)
-    finish(a, a6, x_a, out_a)
-    finish(b, b6, u_b, out_b)
-    links.drain()
+    finish(a, 0, x_a, out_a)
+    finish(a, 1, x_a, out_a)
+    for cls in range(3):
+        links.sent(meta[cls].at[0:3], ("meta1", cls))
+        links.sent(routes[cls].at[0:3], ("meta2", cls))
+    drain(a, "gather1", "gather2", "relay2", "pick", "back1", "back2", "back3")
+    drain(b, "gather1", "gather2", "relay2", "pick", "back1")
+    back3(b, 0)
+    back3(b, 1)
+    finish(b, 0, u_b, out_b)
+    drain(b, "back2")
+    finish(b, 1, u_b, out_b)
+    drain(b, "back3")
 
 
 def deliver(*refs):
@@ -435,7 +466,7 @@
             for shape, dtype in (
                 (lambda w: (SIDE, SIDE, TOK, w), BF16),
                 (lambda w: (SIDE, SIDE, CORES, 16, w), BF16),
-                (lambda w: (SIDE, CORES, SIDE, 16, w), BF16),
+                (lambda w: (SIDE * CORES, SIDE, 16, w), BF16),
                 (lambda w: (SIDE, CORES, SIDE, 16, w), BF16),
                 (lambda w: (SIDE, SIDE, CORES, 16, w), BF16),
                 (lambda w: (SIDE, TOK, w), F32),
@@ -448,6 +479,8 @@
         scratch += [
             pltpu.VMEM((SIDE, CORES, 64, D), BF16),
             pltpu.VMEM((SIDE, CORES, 64, FF), BF16),
+            pltpu.VMEM((2, CORES, HALF, FF), BF16),
+            pltpu.VMEM((3, 3 * COLUMN, SLOTS), BF16),
             pltpu.VMEM((4, HALF, HALF), BF16),
             pltpu.VMEM((TOK, D), F32),
             pltpu.VMEM((TOK, QKV), F32),
@@ -457,8 +490,8 @@
             pltpu.VMEM((FF, D), BF16),
             pltpu.VMEM((2, WO_CHUNK, D), BF16),
             pltpu.VMEM((2, WQ_CHUNK, QKV), BF16),
-            pltpu.SemaphoreType.DMA((N_COPIES,)),
-            pltpu.SemaphoreType.DMA((N_COPIES,)),
+            pltpu.SemaphoreType.DMA((N_PHASES,)),
+            pltpu.SemaphoreType.DMA((N_GROUPS,)),
             pltpu.SemaphoreType.DMA((3,)),
             pltpu.SemaphoreType.DMA((2,)),
             pltpu.SemaphoreType.DMA((2,)),

time: 102 us -> 95.1 us (0.932)
  Pallas kernels: 101 us -> 94.1 us
    pallas_call x1, Pallas kernels: 99.2 us -> 92.2 us  [local_step(): pl.pallas_call(kernel, out_shape=outs, in_specs=[vmem] * 7 + [hbm] * 5, o...]
where the time goes in v3:
time: 95.1 us; the launch traced here: 94.9 us
  Pallas kernels  94.1 us (99%)
    pallas_call x1, Pallas kernels, local_step(): pl.pallas_call(kernel, out_shape=outs, in_specs=[vmem] * 7 + [hbm] * 5, o...  92.2 us
    pallas_call x1, Pallas kernels, local_step(): pl.pallas_call(deliver, out_shape=outs, in_specs=[hbm] * 3, out_specs=(vm...  1.94 us

profile of v3, /device:TPU:0, one launch (start us, length us, event | category | flops | bytes accessed | tf_op | source)
XLA Modules:
  0.0 94.9 jit_solution(13492112524957562497)
XLA Ops:
  0.6 92.2 %moe_pair.1 = (bf16[32,2048]{1,0:T(8,128)(2,1)}, bf16[32,2048]{1,0:T(8,128)(2,1)}, bf16[32,5120]{1,0:T(8,128)(2,1)}) custom-call(bf16[32,2048]{1,0:T(8,128)(2,1)} %refs_0_.1, bf16[32,2048]{1,0:T(8,128)(2,1)} %refs_1_.1, bf16[32,4096]{1,0:T(8,128)(2,1)} %refs_2_.1, s32[8,32]{1,0:T(8,128)} %bitcast.4, s32[8,32]{1,0:T(8,128)} %bitcast.5, f32[8,32]{1,0:T(8,128)} %bitcast.6, ...), custom_call_target="tpu_custom_call" | custom-call | tf_op jit(solution)/shard_map/moe_pair/pallas_call | solution.py:500
  92.8 1.9 %deliver.1 = (bf16[32,2048]{1,0:T(8,128)(2,1)}, bf16[32,2048]{1,0:T(8,128)(2,1)}, bf16[32,5120]{1,0:T(8,128)(2,1)}) custom-call(bf16[32,2048]{1,0:T(8,128)(2,1)} %get-tuple-element.6.refs_0_, bf16[32,2048]{1,0:T(8,128)(2,1)} %get-tuple-element.7.refs_1_, bf16[32,5120]{1,0:T(8,128)(2,1)} %get-tuple-element.8.refs_2_), custom_call_target="tpu_custom_call" | custom-call | tf_op jit(solution)/shard_map/deliver/pallas_call | solution.py:510

commit v4 on v3

--- a/solution.py
+++ b/solution.py
@@ -130,10 +130,6 @@
 
     wo_copy(0).start()
     wo_copy(1).start()
-    for c in w_copies:
-        c.start()
-    wq_copy(0).start()
-    wq_copy(1).start()
 
     def proj_step(i):
         wo_copy(i).wait()
@@ -245,7 +241,7 @@
                 links.copy(ps.at[block, there, there_core], pr.at[CORES * pos[d3] + core, block], first + there_core,
                            ("pick", b["m"], cls))
 
-    def experts(b):
+    def received(b):
         for cls in range(3):
             s, w = b["s"][cls], b["w"][cls]
             pr = b["pr"][cls]
@@ -256,7 +252,8 @@
                     rows = dot(perms[cls - 1], rows).astype(BF16)
                 xbuf[:, c, :, s:s + w] = rows.reshape(SIDE, 64, w)
 
-        @pl.loop(0, FF // 256)
+    def hidden(first, last):
+        @pl.loop(first, last)
         def _(i):
             cols = pl.ds(pl.multiple_of(i * 256, 256), 256)
             x = xbuf[...].reshape(SLOTS, D)
@@ -372,64 +369,66 @@
     pl.semaphore_wait(barrier, len(peers))
     gather1(a, x_a)
     send_meta1()
-    proj_step(0)
-    proj_step(1)
+    for i in range(4):
+        proj_step(i)
     gather2(a)
     send_meta2()
-    proj_step(2)
+    for i in range(4, n_wo):
+        proj_step(i)
+    u_b[...] = (h_b[...].astype(F32) + proj_acc[...].astype(BF16).astype(F32)).astype(BF16)
+    gather1(b, u_b)
+    for c in w_copies:
+        c.start()
+    wq_copy(0).start()
+    wq_copy(1).start()
     for cls in range(3):
         pick(a, cls, 0)
-    proj_step(3)
-    proj_step(4)
+    perms[0] = reorder(0, 1)
+    perms[1] = reorder(0, 2)
     relay2(a)
-    proj_step(5)
     for cls in range(3):
         links.arrived(routes[cls].at[0:3], ("meta2", cls))
         pick(a, cls, 1)
-    proj_step(6)
-    for cls in range(3):
         pick(a, cls, 3)
-    proj_step(7)
-    u_b[...] = (h_b[...].astype(F32) + proj_acc[...].astype(BF16).astype(F32)).astype(BF16)
-    gather1(b, u_b)
+    gather2(b)
     for cls in range(3):
         relayed(a, cls)
         pick(a, cls, 2)
-    gather2(b)
-    perms[0] = reorder(0, 1)
-    perms[1] = reorder(0, 2)
+    for cls in range(3):
+        pick(b, cls, 0)
     perms[2] = reorder(1, 0)
     perms[3] = reorder(2, 0)
-    for cls in range(3):
-        pick(b, cls, 0)
     qkv_step(0)
     relay2(b)
     for cls in range(3):
         pick(b, cls, 1)
         pick(b, cls, 3)
-    qkv_step(1)
+    for c in w_copies:
+        c.wait()
+    received(a)
+    hidden(0, 2)
     for cls in range(3):
         relayed(b, cls)
         pick(b, cls, 2)
-    for c in w_copies:
-        c.wait()
-    experts(a)
+    hidden(2, 3)
     align(a)
     back1(a, 0)
     back1(a, 1)
-    experts(b)
+    qkv_step(1)
+    qkv_step(2)
+    received(b)
+    hidden(0, 3)
     back2(a, 0)
     align(b)
     back1(b, 0)
     back2(a, 1)
     back1(b, 1)
     weigh(a)
-    qkv_step(2)
+    qkv_step(3)
+    back2(b, 0)
     back3(a, 0)
-    back2(b, 0)
-    qkv_step(3)
+    back2(b, 1)
     back3(a, 1)
-    back2(b, 1)
     weigh(b)
     for i in range(4, n_wq):
         qkv_step(i)

time: 95.1 us -> 92.6 us (0.974)
  Pallas kernels: 94.1 us -> 91.6 us
    pallas_call x1, Pallas kernels: 92.2 us -> 89.6 us  [local_step(): pl.pallas_call(kernel, out_shape=outs, in_specs=[vmem] * 7 + [hbm] * 5, o...]
where the time goes in v4:
time: 92.6 us; the launch traced here: 92.4 us
  Pallas kernels  91.6 us (99%)
    pallas_call x1, Pallas kernels, local_step(): pl.pallas_call(kernel, out_shape=outs, in_specs=[vmem] * 7 + [hbm] * 5, o...  89.6 us
    pallas_call x1, Pallas kernels, local_step(): pl.pallas_call(deliver, out_shape=outs, in_specs=[hbm] * 3, out_specs=(vm...  1.94 us

profile of v4, /device:TPU:0, one launch (start us, length us, event | category | flops | bytes accessed | tf_op | source)
XLA Modules:
  0.0 92.4 jit_solution(9584358413130196386)
XLA Ops:
  0.6 89.6 %moe_pair.1 = (bf16[32,2048]{1,0:T(8,128)(2,1)}, bf16[32,2048]{1,0:T(8,128)(2,1)}, bf16[32,5120]{1,0:T(8,128)(2,1)}) custom-call(bf16[32,2048]{1,0:T(8,128)(2,1)} %refs_0_.1, bf16[32,2048]{1,0:T(8,128)(2,1)} %refs_1_.1, bf16[32,4096]{1,0:T(8,128)(2,1)} %refs_2_.1, s32[8,32]{1,0:T(8,128)} %bitcast.4, s32[8,32]{1,0:T(8,128)} %bitcast.5, f32[8,32]{1,0:T(8,128)} %bitcast.6, ...), custom_call_target="tpu_custom_call" | custom-call | tf_op jit(solution)/shard_map/moe_pair/pallas_call | solution.py:499
  90.3 1.9 %deliver.1 = (bf16[32,2048]{1,0:T(8,128)(2,1)}, bf16[32,2048]{1,0:T(8,128)(2,1)}, bf16[32,5120]{1,0:T(8,128)(2,1)}) custom-call(bf16[32,2048]{1,0:T(8,128)(2,1)} %get-tuple-element.6.refs_0_, bf16[32,2048]{1,0:T(8,128)(2,1)} %get-tuple-element.7.refs_1_, bf16[32,5120]{1,0:T(8,128)(2,1)} %get-tuple-element.8.refs_2_), custom_call_target="tpu_custom_call" | custom-call | tf_op jit(solution)/shard_map/deliver/pallas_call | solution.py:509

commit v5 on v4

--- a/solution.py
+++ b/solution.py
@@ -296,7 +296,7 @@
         for cls, (d1, d2, d3) in enumerate(CLASSES):
             r1, r2 = b["r1"][cls], b["r2"][cls]
             lo, hi = lanes(b, cls, part)
-            for off in (0, 1, 3, 2):
+            for off in (2, 0, 1, 3):
                 chip = along(d3, (4 - off) % 4)[0]
                 like = r1.at[0, :, :, :, lo:hi] if off else r1.at[0, 0, :, :, lo:hi]
                 links.arrived(like, ("back1", b["m"], cls), part, off)
@@ -425,10 +425,10 @@
     back1(b, 1)
     weigh(a)
     qkv_step(3)
+    back3(a, 0)
     back2(b, 0)
-    back3(a, 0)
+    back3(a, 1)
     back2(b, 1)
-    back3(a, 1)
     weigh(b)
     for i in range(4, n_wq):
         qkv_step(i)

time: 92.6 us -> 91.5 us (0.988)
  Pallas kernels: 91.6 us -> 90 us
    pallas_call x1, Pallas kernels: 89.6 us -> 88 us  [local_step(): pl.pallas_call(kernel, out_shape=outs, in_specs=[vmem] * 7 + [hbm] * 5, o...]
where the time goes in v5:
time: 91.5 us; the launch traced here: 90.8 us
  Pallas kernels  90 us (98%)
    pallas_call x1, Pallas kernels, local_step(): pl.pallas_call(kernel, out_shape=outs, in_specs=[vmem] * 7 + [hbm] * 5, o...  88 us
    pallas_call x1, Pallas kernels, local_step(): pl.pallas_call(deliver, out_shape=outs, in_specs=[hbm] * 3, out_specs=(vm...  1.94 us

profile of v5, /device:TPU:0, one launch (start us, length us, event | category | flops | bytes accessed | tf_op | source)
XLA Modules:
  0.0 90.8 jit_solution(592122242523429556)
XLA Ops:
  0.6 88.0 %moe_pair.1 = (bf16[32,2048]{1,0:T(8,128)(2,1)}, bf16[32,2048]{1,0:T(8,128)(2,1)}, bf16[32,5120]{1,0:T(8,128)(2,1)}) custom-call(bf16[32,2048]{1,0:T(8,128)(2,1)} %refs_0_.1, bf16[32,2048]{1,0:T(8,128)(2,1)} %refs_1_.1, bf16[32,4096]{1,0:T(8,128)(2,1)} %refs_2_.1, s32[8,32]{1,0:T(8,128)} %bitcast.4, s32[8,32]{1,0:T(8,128)} %bitcast.5, f32[8,32]{1,0:T(8,128)} %bitcast.6, ...), custom_call_target="tpu_custom_call" | custom-call | tf_op jit(solution)/shard_map/moe_pair/pallas_call | solution.py:499
  88.7 1.9 %deliver.1 = (bf16[32,2048]{1,0:T(8,128)(2,1)}, bf16[32,2048]{1,0:T(8,128)(2,1)}, bf16[32,5120]{1,0:T(8,128)(2,1)}) custom-call(bf16[32,2048]{1,0:T(8,128)(2,1)} %get-tuple-element.6.refs_0_, bf16[32,2048]{1,0:T(8,128)(2,1)} %get-tuple-element.7.refs_1_, bf16[32,5120]{1,0:T(8,128)(2,1)} %get-tuple-element.8.refs_2_), custom_call_target="tpu_custom_call" | custom-call | tf_op jit(solution)/shard_map/deliver/pallas_call | solution.py:509
